TPU v7x, 128 devices: a whole 4x4x4 slice. The times are simulated.
128 devices in a mesh: inst: 8 (over y_hi, x), head: 16 (over y_lo, z, core).
Axes of the slice: x: 4, y: 4 (y_hi: 2, y_lo: 2; y = y_hi * 2 + y_lo), z: 4, core: 2. Of those that a mesh axis runs over, the one named last changes fastest.
Arguments:
- old_keys: bfloat16 [1024, 16, 64, 128], P('inst', 'head'), may hold values from -6 to 6
- old_values: bfloat16 [1024, 16, 64, 128], P('inst', 'head'), may hold values from -6 to 6
- old_block: int32 [1024], P('inst'), may hold values from -1 to 255, as said below
- new_slot: int32 [256], replicated, may hold values from 0 to 255, as said below
- lengths: int32 [64], replicated, may hold values from 1 to 16384, as said below
- queries: bfloat16 [64, 16, 8192], P(None, None, 'head'), may hold values from -240 to 240
- draft_keys: bfloat16 [64, 16, 1024], P('inst'), may hold values from -6 to 6
- draft_values: bfloat16 [64, 16, 1024], P('inst'), may hold values from -6 to 6
Outputs:
- moved_keys: bfloat16 [256, 16, 64, 128], P('inst', 'head')
- moved_values: bfloat16 [256, 16, 64, 128], P('inst', 'head')
- attended: bfloat16 [64, 16, 8192], P(None, None, 'head')
Inputs may be any that keep to these rules, and one draw needn't show every extreme that they name: ceil(lengths / 128) summed over the requests is exactly 256; the longest request has exactly 16384 tokens. `old_block`: every block 0 to 255 stands in exactly one old slot; the blocks fill all slots of 2 instances and all other slots hold -1. A permutation; block g goes to instance new_slot[g] // 32. At most 32 blocks go from one old instance to one new one, and in every draw some new instance receives all its 32 blocks from a single old instance.
All inputs are finite; a program needn't handle non-finite values.
Results may differ from a plain program's by a relative error of at most 0.004.
Values may be sent and summed in bfloat16 or wider, within the bound.
No kernel may reach another device: no remote copies, remote signals or barrier semaphores. Data moves between devices by JAX's collectives and lax.ppermute only.
A program may use at most 64 MiB of HBM per device.

v0:
```python
import functools
import math

import jax
import jax.numpy as jnp
from jax import lax
from jax.experimental import pallas as pl
from jax.experimental.pallas import tpu as pltpu
from jax.sharding import PartitionSpec as P


BLK = 128
masked = -1e30


COLS = 4
SENT_K = ((4, 3), (5, 6))
SENT_V = ((5,), (3,), (7,))
KEPT_K = ((2,), (7,), (0,), (1,))
KEPT_V = ((1,), (4,), (2,), (6,), (0,))


def pack_body(groups_k, groups_v, old_block, new_slot, base, keys, values, *rest):
    count = len(groups_k) + len(groups_v)
    outs = rest[:count]
    vk, vv, zeros, origin, sems, load_sem = rest[count:]
    slots = keys.shape[0]
    total = new_slot.shape[0]
    per = zeros.shape[0]
    is_source = old_block[0] >= 0
    jobs = [(vk, out, group) for out, group in zip(outs, groups_k)]
    jobs += [(vv, out, group) for out, group in zip(outs[len(groups_k) :], groups_v)]
    places = {}
    for at, (cache, out, group) in enumerate(jobs):
        for g, p in enumerate(group):
            places.setdefault(p, []).append((cache, out, at, g * per))

    @pl.when(is_source)
    def _():
        load_k = pltpu.make_async_copy(keys, vk.at[pl.ds(0, slots)], load_sem.at[0])
        load_v = pltpu.make_async_copy(values, vv.at[pl.ds(0, slots)], load_sem.at[1])
        load_k.start()
        load_v.start()
        vk[slots] = jnp.zeros(zeros.shape[1:], zeros.dtype)
        vv[slots] = jnp.zeros(zeros.shape[1:], zeros.dtype)

        def clear(t, c):
            origin[t] = slots
            return c

        lax.fori_loop(0, total, clear, 0, unroll=16)

        def note(i, c):
            origin[new_slot[jnp.maximum(old_block[i], 0)]] = i
            return c

        lax.fori_loop(0, slots, note, 0, unroll=16)
        load_k.wait()
        load_v.wait()
        for p in sorted(places):
            start = base[p]

            def send(j, c, p=p, start=start):
                i = origin[start + j]
                for cache, out, at, first in places[p]:
                    pltpu.make_async_copy(cache.at[i], out.at[first + j], sems.at[at]).start()
                return c

            lax.fori_loop(0, per, send, 0, unroll=8)

    @pl.when(jnp.logical_not(is_source))
    def _():
        zeros[...] = jnp.zeros(zeros.shape, zeros.dtype)
        for at, (cache, out, group) in enumerate(jobs):
            for g in range(len(group)):
                pltpu.make_async_copy(zeros, out.at[pl.ds(g * per, per)], sems.at[at]).start()

    for at, (cache, out, group) in enumerate(jobs):
        pltpu.make_async_copy(out, out, sems.at[at]).wait()


def table_of(per, rows, half, head_dim):
    insts = lax.axis_size("inst")
    inst = lax.axis_index("inst")
    me_head = lax.axis_index("head")
    step = jnp.arange(16, dtype=jnp.int32)
    away = (inst // COLS) ^ (step % 2)
    column = (inst % COLS + step // 2) % COLS
    base = (away * COLS + column) * per
    rest = jnp.where(
        step == insts,
        inst * rows,
        jnp.where(step == insts + 1, me_head % 2 * half, me_head // 2 * head_dim),
    )
    return jnp.where(step < insts, base, rest)


def pack(old_block, new_slot, base, keys, values, insts, groups_k, groups_v):
    total = new_slot.shape[0]
    per = total // insts
    groups = groups_k + groups_v
    anyspace = pl.BlockSpec(memory_space=pl.ANY)
    smem = pl.BlockSpec(memory_space=pltpu.SMEM)
    got = pl.pallas_call(
        functools.partial(pack_body, groups_k, groups_v),
        in_specs=[smem, smem, smem, anyspace, anyspace],
        out_specs=[anyspace] * len(groups),
        out_shape=[
            jax.ShapeDtypeStruct((per * len(g),) + keys.shape[1:], keys.dtype) for g in groups
        ],
        scratch_shapes=[
            pltpu.VMEM((keys.shape[0] + 1,) + keys.shape[1:], keys.dtype),
            pltpu.VMEM((keys.shape[0] + 1,) + keys.shape[1:], keys.dtype),
            pltpu.VMEM((per,) + keys.shape[1:], keys.dtype),
            pltpu.SMEM((total,), jnp.int32),
            pltpu.SemaphoreType.DMA((len(groups),)),
            pltpu.SemaphoreType.DMA((2,)),
        ],
    )(old_block, new_slot, base, keys, values)
    return got[: len(groups_k)], got[len(groups_k) :]


def right(x):
    rows = lax.axis_size("inst") // COLS
    route = [(r * COLS + c, r * COLS + (c + 1) % COLS) for r in range(rows) for c in range(COLS)]
    return lax.ppermute(x, "inst", route)


def left(x):
    rows = lax.axis_size("inst") // COLS
    route = [(r * COLS + (c + 1) % COLS, r * COLS + c) for r in range(rows) for c in range(COLS)]
    return lax.ppermute(x, "inst", route)


def across(x):
    return lax.ppermute(x, "inst", [(i, i ^ COLS) for i in range(lax.axis_size("inst"))])


def move_keys(from_left, from_right, groups):
    k1n, k3f, k0n, k0f = groups
    per = k1n.shape[0]
    a2 = right(k1n + from_left[:per])
    b2 = left(k3f + from_right[:per])
    b2, from_left = lax.optimization_barrier((b2, from_left))
    crossed = across(k0f + from_left[per:] + b2)
    return k0n + from_right[per:] + a2 + crossed


def move_values(got2, got1, got3, y0, groups):
    v2n, v1n, v3n, v0n = groups
    per = v1n.shape[0]
    cut = per // 2
    from_left = right(v2n[:cut] + got2[:cut])
    from_right = left(v2n[cut:] + got2[cut:])
    rest = jnp.zeros((per - cut,) + v1n.shape[1:], v1n.dtype)
    a2 = right(v1n + got1 + jnp.concatenate([from_left, rest]))
    b2 = left(v3n + got3 + jnp.concatenate([rest, from_right]))
    return v0n + y0 + a2 + b2


def dot_t(x, y):
    return lax.dot_general(x, y, (((1,), (1,)), ((), ())), preferred_element_type=jnp.float32)


def attend_body(
    old_block, lengths, meta, q, k, v, ok, ov, dks, dvs, packet,
    vq, dk, dv, vk, vv, vok, vov, scores, drafted, peak, total, acc, owner, live, sems,
):
    requests, draft, width = vq.shape
    head_dim = vk.shape[2]
    half = vk.shape[1]
    slots = vk.shape[0]
    heads = width // head_dim
    qrows = draft * heads
    insts = packet.shape[0]
    rows = requests // insts
    inv_root = 1.0 / math.sqrt(head_dim)
    is_source = old_block[0] >= 0
    first = meta[insts]
    shift = meta[insts + 1]
    kv = pl.ds(pl.multiple_of(meta[insts + 2], head_dim), head_dim)
    early = [
        pltpu.make_async_copy(q, vq, sems.at[0]),
        pltpu.make_async_copy(dks.at[:, :, kv], dk, sems.at[5]),
        pltpu.make_async_copy(dvs.at[:, :, kv], dv, sems.at[6]),
    ]
    for load in early:
        load.start()
    loads = [
        pltpu.make_async_copy(x, y, sems.at[1 + n])
        for n, (x, y) in enumerate(((k, vk), (ok, vok), (v, vv), (ov, vov)))
    ]

    @pl.when(is_source)
    def _():
        for load in loads:
            load.start()

        def per_request(r, g):
            size = lengths[r]

            def per_block(j, c):
                owner[g + j] = r
                live[g + j] = jnp.minimum(size - j * BLK, BLK)
                return c

            n = (size + BLK - 1) // BLK
            lax.fori_loop(0, n, per_block, 0)
            return g + n

        lax.fori_loop(0, requests, per_request, 0)

    def q_of(r):
        return jnp.concatenate(
            [vq[r, :, h * head_dim : (h + 1) * head_dim] for h in range(heads)], axis=0
        )

    lane = lax.broadcasted_iota(jnp.int32, (qrows, head_dim), 1)
    row = lax.broadcasted_iota(jnp.int32, (qrows, head_dim), 0)
    place = (lane + shift) % (2 * half)
    fold = head_dim // heads
    causal = lane <= row % draft
    blank = jnp.full((qrows, head_dim), masked, jnp.float32)

    def reset(r, c):
        peak[r] = blank
        return c

    lax.fori_loop(0, requests, reset, 0, unroll=4)
    for load in early:
        load.wait()
    pad = jnp.zeros((2 * half - draft, head_dim), dk.dtype)
    for a in range(rows):
        s = dot_t(q_of(first + a), jnp.concatenate([dk[a], pad], axis=0)) * inv_root
        s = jnp.where(causal, s, masked)
        drafted[a] = s
        peak[first + a] = s

    @pl.when(is_source)
    def _():
        loads[0].wait()
        loads[1].wait()

        def score(n, c):
            found = []
            for u in range(UNROLL):
                i = n * UNROLL + u
                g = jnp.maximum(old_block[i], 0)
                r = owner[g]
                key = jnp.concatenate([vk[i], vok[i]], axis=0)
                s = dot_t(q_of(r), key) * inv_root
                found.append((i, r, jnp.where(place < live[g], s, masked)))
            for i, r, s in found:
                scores[i] = s
                peak[r] = jnp.maximum(peak[r], s)
            return c

        lax.fori_loop(0, slots // UNROLL, score, 0)

    def settle(r, c):
        peak[r] = jnp.broadcast_to(jnp.max(peak[r], axis=1, keepdims=True), (qrows, head_dim))
        total[r] = jnp.zeros((qrows, head_dim), jnp.float32)
        acc[r] = jnp.zeros((qrows, head_dim), jnp.float32)
        return c

    lax.fori_loop(0, requests, settle, 0, unroll=SETTLE)
    for a in range(rows):
        w = jnp.exp(drafted[a] - peak[first + a])
        total[first + a] = w
        acc[first + a] = jnp.dot(
            w.astype(dv.dtype),
            jnp.concatenate([dv[a], pad], axis=0),
            preferred_element_type=jnp.float32,
        )

    @pl.when(is_source)
    def _():
        loads[2].wait()
        loads[3].wait()

        def gather(n, c):
            found = []
            for u in range(UNROLL):
                i = n * UNROLL + u
                r = owner[jnp.maximum(old_block[i], 0)]
                w = jnp.exp(scores[i] - peak[r])
                value = jnp.concatenate([vv[i], vov[i]], axis=0)
                out = jnp.dot(w.astype(vv.dtype), value, preferred_element_type=jnp.float32)
                found.append((r, w, out))
            for r, w, out in found:
                total[r] += w
                acc[r] += out
            return c

        lax.fori_loop(0, slots // UNROLL, gather, 0)

    def finish(d, c):
        sums = jnp.zeros((qrows, head_dim), jnp.float32)
        tops = jnp.zeros((qrows, head_dim), jnp.float32)
        for a in range(rows):
            r = d * rows + a
            l = jnp.sum(total[r], axis=1, keepdims=True)
            scale = 1.0 / jnp.where(l > 0, l, 1.0)
            packet[d, a * qrows : (a + 1) * qrows, :] = (acc[r] * scale).astype(packet.dtype)
            sums = jnp.where(lane % rows == a, l, sums)
            tops = jnp.where(lane % rows == a, peak[r], tops)
        level = jnp.where(sums > 0, tops + jnp.log(jnp.where(sums > 0, sums, 1.0)), masked)
        hi = level.astype(jnp.bfloat16).astype(jnp.float32)
        mid = (level - hi).astype(jnp.bfloat16).astype(jnp.float32)
        stat = jnp.where(lane < rows, hi, jnp.where(lane < 2 * rows, mid, level - hi - mid))
        stat = jnp.where(lane < 3 * rows, stat, 0.0)
        folded = stat[:draft]
        for h in range(1, heads):
            folded += pltpu.roll(stat[h * draft : (h + 1) * draft], h * fold, 1)
        packet[d, rows * qrows :, :] = folded.astype(packet.dtype)
        return c

    lax.fori_loop(0, insts, finish, 0)


UNROLL = 32
SETTLE = 16


def attend(old_block, lengths, meta, queries, keys, values, other_k, other_v, dk, dv, insts):
    requests, draft, width = queries.shape
    head_dim = keys.shape[2]
    qrows = draft * width // head_dim
    rows = requests // insts
    anyspace = pl.BlockSpec(memory_space=pl.ANY)
    smem = pl.BlockSpec(memory_space=pltpu.SMEM)
    vmem = pl.BlockSpec(memory_space=pltpu.VMEM)
    bf16 = jnp.bfloat16
    state = pltpu.VMEM((requests, qrows, head_dim), jnp.float32)
    return pl.pallas_call(
        attend_body,
        in_specs=[smem] * 3 + [anyspace] * 7,
        out_specs=vmem,
        out_shape=jax.ShapeDtypeStruct((insts, rows * qrows + draft, head_dim), bf16),
        scratch_shapes=[pltpu.VMEM(queries.shape, bf16)]
        + [pltpu.VMEM((rows, draft, head_dim), bf16)] * 2
        + [pltpu.VMEM(keys.shape, bf16)] * 4
        + [
            pltpu.VMEM((keys.shape[0], qrows, head_dim), jnp.float32),
            pltpu.VMEM((rows, qrows, head_dim), jnp.float32),
            state,
            state,
            state,
            pltpu.SMEM((TOTAL,), jnp.int32),
            pltpu.SMEM((TOTAL,), jnp.int32),
            pltpu.SemaphoreType.DMA((7,)),
        ],
        name="attend",
    )(old_block, lengths, meta, queries, keys, values, other_k, other_v, dk, dv)


TOTAL = 256


def join_body(arrived, out, got, sem):
    load = pltpu.make_async_copy(arrived, got, sem)
    load.start()
    insts, _, head_dim = got.shape
    rows = out.shape[1]
    draft = out.shape[2]
    heads = out.shape[3] // head_dim
    qrows = draft * heads
    fold = head_dim // heads
    lane = lax.broadcasted_iota(jnp.int32, (draft, head_dim), 1)
    load.wait()
    stats = [got[s, rows * qrows :, :].astype(jnp.float32) for s in range(insts)]
    for a in range(rows):
        mine = [
            (lane % rows == a) & (lane >= h * fold) & (lane < h * fold + 3 * rows)
            for h in range(heads)
        ]
        level = [
            jnp.concatenate(
                [jnp.sum(jnp.where(m, stat, 0.0), axis=1, keepdims=True) for m in mine], axis=0
            )
            for stat in stats
        ]
        top = level[0]
        for x in level[1:]:
            top = jnp.maximum(top, x)
        total = jnp.zeros((qrows, 1), jnp.float32)
        acc = jnp.zeros((qrows, head_dim), jnp.float32)
        for s in range(insts):
            share = jnp.exp(level[s] - top)
            total = total + share
            acc = acc + share * got[s, a * qrows : (a + 1) * qrows, :].astype(jnp.float32)
        res = (acc / total).astype(out.dtype)
        for d in range(insts):
            for h in range(heads):
                out[d, a, :, h * head_dim : (h + 1) * head_dim] = res[h * draft : (h + 1) * draft]


def join(got, rows, draft, width):
    insts = got.shape[0]
    vmem = pl.BlockSpec(memory_space=pltpu.VMEM)
    return pl.pallas_call(
        join_body,
        in_specs=[pl.BlockSpec(memory_space=pl.ANY)],
        out_specs=vmem,
        out_shape=jax.ShapeDtypeStruct((insts, rows, draft, width), got.dtype),
        scratch_shapes=[pltpu.VMEM(got.shape, got.dtype), pltpu.SemaphoreType.DMA],
        name="join",
    )(got)


def spread(x):
    return lax.all_to_all(x, "inst", split_axis=0, concat_axis=0, tiled=True)


def move_and_attend(
    old_keys, old_values, old_block, new_slot, lengths, queries, draft_keys, draft_values
):
    insts = lax.axis_size("inst")
    _, entries, half, head_dim = old_keys.shape
    keys = old_keys.reshape(-1, half, head_dim)
    values = old_values.reshape(-1, half, head_dim)
    blocks = new_slot.shape[0]
    requests = queries.shape[0]
    rows = requests // insts
    swap = [(i, i ^ 1) for i in range(lax.axis_size("head"))]
    other_k = lax.ppermute(keys, "head", swap)
    other_v = lax.ppermute(values, "head", swap)

    table = table_of(blocks // insts, rows, half, head_dim)
    out_k, out_v = pack(
        old_block, new_slot, table, keys, values, insts, SENT_K + KEPT_K, SENT_V + KEPT_V
    )
    queries, out_k, out_v = lax.optimization_barrier((queries, out_k, out_v))
    shape = (blocks // insts, entries, half, head_dim)
    far2 = across(out_v[0])
    from_left = right(out_k[0])
    from_right = left(out_k[1])
    far1 = across(out_v[1])
    far3 = across(out_v[2])
    kept_k, kept_v = out_k[len(SENT_K) :], out_v[len(SENT_V) :]
    near = across(kept_v[0])
    packet = attend(
        old_block, lengths, table, queries, keys, values, other_k, other_v,
        draft_keys, draft_values, insts,
    )
    packet, rest_k, rest_v = lax.optimization_barrier((packet, kept_k, kept_v[1:]))
    moved_keys = move_keys(from_left, from_right, rest_k).reshape(shape)
    moved_values = move_values(far2, far1, far3, near, rest_v).reshape(shape)
    got = spread(packet)
    mine = join(got, rows, queries.shape[1], queries.shape[2])
    attended = spread(mine).reshape(queries.shape)
    return moved_keys, moved_values, attended


def solution(mesh):
    placed = (
        P("inst", "head", None, None),
        P("inst", "head", None, None),
        P("inst"),
        P(),
        P(),
        P(None, None, "head"),
        P("inst", None, None),
        P("inst", None, None),
    )
    return jax.shard_map(
        move_and_attend,
        mesh=mesh,
        in_specs=placed,
        out_specs=(
            P("inst", "head", None, None),
            P("inst", "head", None, None),
            P(None, None, "head"),
        ),
        check_vma=False,
    )
```

profile of v0, /device:TPU:0, one launch (start us, length us, event | category | flops | bytes accessed | tf_op | source)
XLA Modules:
  0.0 115.0 jit_solution(15157380905458781263)
XLA Ops:
  0.6 0.1 collective-permute-start
  0.7 0.5 collective-permute-start.1
  1.2 0.5 compare_select_fusion.4.base.meta
  1.8 4.2 %shard_map.103 = (bf16[64,64,128]{2,1,0:T(8,128)(2,1)}, bf16[64,64,128]{2,1,0:T(8,128)(2,1)}, bf16[32,64,128]{2,1,0:T(8,128)(2,1)}, bf16[32,64,128]{2,1,0:T(8,12...) custom-call(s32[128]{0:T(128)} %old_block.3, ...), custom_call_target="tpu_custom_call" | custom-call | tf_op jit(solution)/shard_map/pallas_call | solution.py:104
  6.0 2.9 %collective-permute-start.2 = (bf16[64,64,128]{2,1,0:T(8,128)(2,1)}, bf16[64,64,128]{2,1,0:T(8,128)(2,1)S(1)}, u32[]{:S(2)}, u32[]{:S(2)}) collective-permute-start(bf16[64,64,128]{2,1,0:T(8,128)(2,1)} %get-tuple-element.67), channel_id=1, source_target_pairs={{16,0},{32,16},{48,32},{0,48},{80,64},{96,80},{112,96},{64,112},{1... | collective-permute-start | bytes 3145736 | tf_op jit(solution)/shard_map/ppermute | solution.py:132
  9.0 3.2 %collective-permute-start.9 = (bf16[32,64,128]{2,1,0:T(8,128)(2,1)}, bf16[32,64,128]{2,1,0:T(8,128)(2,1)}, u32[]{:S(2)}, u32[]{:S(2)}) collective-permute-start(bf16[32,64,128]{2,1,0:T(8,128)(2,1)} %get-tuple-element.79), channel_id=1, source_target_pairs={{0,64},{16,80},{32,96},{48,112},{64,0},{80,16},{96,32},{112,48},{1... | collective-permute-start | bytes 1572872 | tf_op jit(solution)/shard_map/ppermute | solution.py:136
  12.2 0.3 collective-permute-start.8
  12.5 0.0 collective-permute-done.ok
  12.5 1.0 collective-permute-start.3
  13.5 0.0 collective-permute-done.1.ov
  13.5 3.5 %collective-permute-start.7 = (bf16[32,64,128]{2,1,0:T(8,128)(2,1)}, bf16[32,64,128]{2,1,0:T(8,128)(2,1)}, u32[]{:S(2)}, u32[]{:S(2)}) collective-permute-start(bf16[32,64,128]{2,1,0:T(8,128)(2,1)} %get-tuple-element.75), channel_id=1, source_target_pairs={{0,64},{16,80},{32,96},{48,112},{64,0},{80,16},{96,32},{112,48},{1... | collective-permute-start | bytes 1572872 | tf_op jit(solution)/shard_map/ppermute | solution.py:136
  16.9 5.9 %attend.1 = bf16[8,528,128]{2,1,0:T(8,128)(2,1)} custom-call(s32[128]{0:T(128)} %old_block.3, s32[64]{0:T(128)} %lengths.1, s32[16]{0:T(128)} %compare_select_fusion.4.base.meta, bf16[64,16,512]{2,1,0:T(8,128)(2,1)} %q, bf16[128,64,128]{2,1,0:T(8,128)(2,1)} %bitcast.13, bf16[128,64,128]{2,1,0:T(8,128)(2,1)} %bitcast.16, bf16[128,64,128]{2,1,0:T(8,128)(2,1)} %copy-done.1, ...), custom_call_target="tpu_custom_call" | custom-call | tf_op jit(solution)/shard_map/attend/pallas_call | solution.py:335
  22.8 0.0 copy-start.7
  22.8 8.2 %all-to-all-start = ((bf16[8,528,128]{2,1,0:T(8,128)(2,1)}), bf16[8,528,128]{2,1,0:T(8,128)(2,1)S(1)}, u32[]{:S(2)}, u32[]{:S(2)}) async-start(bf16[8,528,128]{2,1,0:T(8,128)(2,1)} %attend.1), calls=%async_computation | async-start | bytes 2162688 | tf_op jit(solution)/shard_map/all_to_all | solution.py:412
  31.1 0.0 collective-permute-done.9
  31.1 3.6 %collective-permute-start.12 = (bf16[32,64,128]{2,1,0:T(8,128)(2,1)}, bf16[32,64,128]{2,1,0:T(8,128)(2,1)S(1)}, u32[]{:S(2)}, u32[]{:S(2)}) collective-permute-start(bf16[32,64,128]{2,1,0:T(8,128)(2,1)} %get-tuple-element.81), channel_id=1, source_target_pairs={{0,64},{16,80},{32,96},{48,112},{64,0},{80,16},{96,32},{112,48},{1... | collective-permute-start | bytes 1572872 | tf_op jit(solution)/shard_map/ppermute | solution.py:136
  34.7 1.2 %slice_add_fusion.4 = (bf16[16,64,128]{2,1,0:T(8,128)(2,1)S(1)}, bf16[16,64,128]{2,1,0:T(8,128)(2,1)S(1)}) fusion(bf16[32,64,128]{2,1,0:T(8,128)(2,1)} %collective-permute-done.9, bf16[32,64,128]{2,1,0:T(8,128)(2,1)} %get-tuple-element.78), kind=kLoop, calls=%fused_computation.11 | loop fusion | flops 262144 | bytes 1572864 | tf_op jit(solution)/shard_map/add | solution.py:153
  35.9 0.0 collective-permute-done.2
  36.0 1.5 %collective-permute-start.10 = (bf16[16,64,128]{2,1,0:T(8,128)(2,1)S(1)}, bf16[16,64,128]{2,1,0:T(8,128)(2,1)S(1)}, u32[]{:S(2)}, u32[]{:S(2)}) collective-permute-start(bf16[16,64,128]{2,1,0:T(8,128)(2,1)S(1)} %get-tuple-element.86), channel_id=1, source_target_pairs={{0,16},{16,32},{32,48},{48,0},{64,80},{80,96},{96,112},{112,64},{1... | collective-permute-start | bytes 786440 | tf_op jit(solution)/shard_map/ppermute | solution.py:126
  37.5 0.1 slice_add_fusion
  37.5 0.0 copy-start.4
  37.6 0.0 collective-permute-done.8
  37.6 2.3 %collective-permute-start.13 = (bf16[16,64,128]{2,1,0:T(8,128)(2,1)S(1)}, bf16[16,64,128]{2,1,0:T(8,128)(2,1)S(1)}, u32[]{:S(2)}, u32[]{:S(2)}) collective-permute-start(bf16[16,64,128]{2,1,0:T(8,128)(2,1)S(1)} %get-tuple-element.87), channel_id=1, source_target_pairs={{16,0},{32,16},{48,32},{0,48},{80,64},{96,80},{112,96},{64,112},{1... | collective-permute-start | bytes 786440 | tf_op jit(solution)/shard_map/ppermute | solution.py:132
  39.8 15.6 %collective-permute-done.10 = bf16[16,64,128]{2,1,0:T(8,128)(2,1)S(1)} collective-permute-done((bf16[16,64,128]{2,1,0:T(8,128)(2,1)S(1)}, bf16[16,64,128]{2,1,0:T(8,128)(2,1)S(1)}, u32[]{:S(2)}, u32[]{:S(2)}) %collective-permute-start.10) | collective-permute-done | bytes 262176 | tf_op jit(solution)/shard_map/ppermute | solution.py:126
  55.5 0.4 collective-permute-start.5
  55.9 1.9 %pad_add_fusion.1 = bf16[32,64,128]{2,1,0:T(8,128)(2,1)} fusion(bf16[16,64,128]{2,1,0:T(8,128)(2,1)S(1)} %collective-permute-done.10, bf16[32,64,128]{2,1,0:T(8,128)(2,1)S(1)} %copy-done.6, bf16[32,64,128]{2,1,0:T(8,128)(2,1)} %collective-permute-done.8), kind=kLoop, calls=%fused_computation.8 | loop fusion | flops 524288 | bytes 1835008 | tf_op jit(solution)/shard_map/add | solution.py:156
  57.8 11.8 %collective-permute-done.12 = bf16[32,64,128]{2,1,0:T(8,128)(2,1)S(1)} collective-permute-done((bf16[32,64,128]{2,1,0:T(8,128)(2,1)}, bf16[32,64,128]{2,1,0:T(8,128)(2,1)S(1)}, u32[]{:S(2)}, u32[]{:S(2)}) %collective-permute-start.12) | collective-permute-done | bytes 524320 | tf_op jit(solution)/shard_map/ppermute | solution.py:136
  69.6 1.2 %collective-permute-start.11 = (bf16[32,64,128]{2,1,0:T(8,128)(2,1)}, bf16[32,64,128]{2,1,0:T(8,128)(2,1)}, u32[]{:S(2)}, u32[]{:S(2)}) collective-permute-start(bf16[32,64,128]{2,1,0:T(8,128)(2,1)} %pad_add_fusion.1), channel_id=1, source_target_pairs={{0,16},{16,32},{32,48},{48,0},{64,80},{80,96},{96,112},{112,64},{1... | collective-permute-start | bytes 1572872 | tf_op jit(solution)/shard_map/ppermute | solution.py:126
  70.8 0.0 collective-permute-done.13
  70.8 0.9 pad_add_fusion
  71.7 2.0 %collective-permute-start.14 = (bf16[32,64,128]{2,1,0:T(8,128)(2,1)}, bf16[32,64,128]{2,1,0:T(8,128)(2,1)}, u32[]{:S(2)}, u32[]{:S(2)}) collective-permute-start(bf16[32,64,128]{2,1,0:T(8,128)(2,1)} %pad_add_fusion), channel_id=1, source_target_pairs={{16,0},{32,16},{48,32},{0,48},{80,64},{96,80},{112,96},{64,112},{1... | collective-permute-start | bytes 1572872 | tf_op jit(solution)/shard_map/ppermute | solution.py:132
  73.7 0.0 collective-permute-done.3
  73.7 1.9 %slice_add_fusion.1 = bf16[32,64,128]{2,1,0:T(8,128)(2,1)} fusion(bf16[32,64,128]{2,1,0:T(8,128)(2,1)S(1)} %copy-done.4, bf16[64,64,128]{2,1,0:T(8,128)(2,1)} %collective-permute-done.3), kind=kLoop, calls=%fused_computation.1 | loop fusion | flops 262144 | bytes 1572864 | tf_op jit(solution)/shard_map/add | solution.py:142
  75.6 0.0 collective-permute-start.4
  75.6 0.0 collective-permute-done.5
  75.6 0.0 all-to-all-done.arrived
  75.7 1.0 copy-done
  76.7 3.5 %join.1 = bf16[8,8,16,512]{3,2,1,0:T(8,128)(2,1)} custom-call(bf16[8,528,128]{2,1,0:T(8,128)(2,1)} %copy-done), custom_call_target="tpu_custom_call" | custom-call | tf_op jit(solution)/shard_map/join/pallas_call | solution.py:401
  80.2 7.3 %all-to-all-start.1 = ((bf16[8,8,16,512]{3,2,1,0:T(8,128)(2,1)}), bf16[8,8,16,512]{3,2,1,0:T(8,128)(2,1)S(1)}, u32[]{:S(2)}, u32[]{:S(2)}) async-start(bf16[8,8,16,512]{3,2,1,0:T(8,128)(2,1)} %join.1), calls=%async_computation.1 | async-start | bytes 2097152 | tf_op jit(solution)/shard_map/all_to_all | solution.py:412
  87.5 1.5 %add_add_fusion = bf16[32,64,128]{2,1,0:T(8,128)(2,1)S(1)} fusion(bf16[32,64,128]{2,1,0:T(8,128)(2,1)} %collective-permute-done.5, bf16[32,64,128]{2,1,0:T(8,128)(2,1)} %get-tuple-element.70, bf16[64,64,128]{2,1,0:T(8,128)(2,1)} %collective-permute-done.3), kind=kLoop, calls=%fused_computation.9 | loop fusion | flops 524288 | bytes 2097152 | tf_op jit(solution)/shard_map/add | solution.py:145
  89.0 3.6 %collective-permute-start.6 = (bf16[32,64,128]{2,1,0:T(8,128)(2,1)S(1)}, bf16[32,64,128]{2,1,0:T(8,128)(2,1)S(1)}, u32[]{:S(2)}, u32[]{:S(2)}) collective-permute-start(bf16[32,64,128]{2,1,0:T(8,128)(2,1)S(1)} %add_add_fusion), channel_id=1, source_target_pairs={{0,64},{16,80},{32,96},{48,112},{64,0},{80,16},{96,32},{112,48},{1... | collective-permute-start | bytes 1572872 | tf_op jit(solution)/shard_map/ppermute | solution.py:136
  92.6 0.0 collective-permute-done.7
  92.6 2.3 %add_bitcast_fusion = bf16[32,1,64,128]{3,2,1,0:T(8,128)(2,1)} fusion(bf16[32,64,128]{2,1,0:T(8,128)(2,1)} %collective-permute-done.14, bf16[32,64,128]{2,1,0:T(8,128)(2,1)} %collective-permute-done.11, bf16[32,64,128]{2,1,0:T(8,128)(2,1)S(1)} %copy-done.3, bf16[32,64,128]{2,1,0:T(8,128)(2,1)} %collective-permute-done.7), kind=kLoop, calls=%fused_computation.6 | loop fusion | flops 786432 | bytes 2621440
  94.8 7.9 %collective-permute-done.4 = bf16[32,64,128]{2,1,0:T(8,128)(2,1)} collective-permute-done((bf16[32,64,128]{2,1,0:T(8,128)(2,1)}, bf16[32,64,128]{2,1,0:T(8,128)(2,1)}, u32[]{:S(2)}, u32[]{:S(2)}) %collective-permute-start.4) | collective-permute-done | bytes 524320 | tf_op jit(solution)/shard_map/ppermute | solution.py:126
  102.8 9.3 %collective-permute-done.6 = bf16[32,64,128]{2,1,0:T(8,128)(2,1)S(1)} collective-permute-done((bf16[32,64,128]{2,1,0:T(8,128)(2,1)S(1)}, bf16[32,64,128]{2,1,0:T(8,128)(2,1)S(1)}, u32[]{:S(2)}, u32[]{:S(2)}) %collective-permute-start.6) | collective-permute-done | bytes 524320 | tf_op jit(solution)/shard_map/ppermute | solution.py:136
  112.1 1.9 %fusion.2 = bf16[32,1,64,128]{3,2,1,0:T(8,128)(2,1)} fusion(bf16[32,64,128]{2,1,0:T(8,128)(2,1)S(1)} %collective-permute-done.6, bf16[32,64,128]{2,1,0:T(8,128)(2,1)} %collective-permute-done.4, bf16[32,64,128]{2,1,0:T(8,128)(2,1)S(1)} %copy-done.2, bf16[64,64,128]{2,1,0:T(8,128)(2,1)S(1)} %collective-permute-done.2), kind=kLoop, calls=%fused_computation.5 | loop fusion | flops 786432 | bytes 2621440
  114.0 0.0 all-to-all-done.1
  114.0 1.0 copy.14
  (15 shorter events, 0.0 us)
Async XLA Ops:
  0.6 11.9 %collective-permute-start = (bf16[128,64,128]{2,1,0:T(8,128)(2,1)}, bf16[128,64,128]{2,1,0:T(8,128)(2,1)S(1)}, u32[]{:S(2)}, u32[]{:S(2)}) collective-permute-start(bf16[128,64,128]{2,1,0:T(8,128)(2,1)} %bitcast.11), channel_id=1, source_target_pairs={{0,1},{1,0},{2,3},{3,2},{4,5},{5,4},{6,7},{7,6},{8,9},{9,8},{10,11... | collective-permute-start | bytes 6291464 | tf_op jit(solution)/shard_map/ppermute | solution.py:426
  0.7 12.8 %collective-permute-start.1 = (bf16[128,64,128]{2,1,0:T(8,128)(2,1)}, bf16[128,64,128]{2,1,0:T(8,128)(2,1)}, u32[]{:S(2)}, u32[]{:S(2)}) collective-permute-start(bf16[128,64,128]{2,1,0:T(8,128)(2,1)} %bitcast.14), channel_id=1, source_target_pairs={{0,1},{1,0},{2,3},{3,2},{4,5},{5,4},{6,7},{7,6},{8,9},{9,8},{10,11... | collective-permute-start | bytes 6291464 | tf_op jit(solution)/shard_map/ppermute | solution.py:427
  6.0 29.9 %collective-permute-start.2 = (bf16[64,64,128]{2,1,0:T(8,128)(2,1)}, bf16[64,64,128]{2,1,0:T(8,128)(2,1)S(1)}, u32[]{:S(2)}, u32[]{:S(2)}) collective-permute-start(bf16[64,64,128]{2,1,0:T(8,128)(2,1)} %get-tuple-element.67), channel_id=1, source_target_pairs={{16,0},{32,16},{48,32},{0,48},{80,64},{96,80},{112,96},{64,112},{1... | collective-permute-start | bytes 3145736 | tf_op jit(solution)/shard_map/ppermute | solution.py:132
  9.0 22.1 %collective-permute-start.9 = (bf16[32,64,128]{2,1,0:T(8,128)(2,1)}, bf16[32,64,128]{2,1,0:T(8,128)(2,1)}, u32[]{:S(2)}, u32[]{:S(2)}) collective-permute-start(bf16[32,64,128]{2,1,0:T(8,128)(2,1)} %get-tuple-element.79), channel_id=1, source_target_pairs={{0,64},{16,80},{32,96},{48,112},{64,0},{80,16},{96,32},{112,48},{1... | collective-permute-start | bytes 1572872 | tf_op jit(solution)/shard_map/ppermute | solution.py:136
  12.2 25.4 %collective-permute-start.8 = (bf16[32,64,128]{2,1,0:T(8,128)(2,1)}, bf16[32,64,128]{2,1,0:T(8,128)(2,1)}, u32[]{:S(2)}, u32[]{:S(2)}) collective-permute-start(bf16[32,64,128]{2,1,0:T(8,128)(2,1)} %get-tuple-element.77), channel_id=1, source_target_pairs={{0,64},{16,80},{32,96},{48,112},{64,0},{80,16},{96,32},{112,48},{1... | collective-permute-start | bytes 1572872 | tf_op jit(solution)/shard_map/ppermute | solution.py:136
  12.5 4.5 %copy-start.1 = (bf16[128,64,128]{2,1,0:T(8,128)(2,1)}, bf16[128,64,128]{2,1,0:T(8,128)(2,1)S(1)}, u32[]{:S(2)}) copy-start(bf16[128,64,128]{2,1,0:T(8,128)(2,1)S(1)} %collective-permute-done.ok) | copy-start | bytes 6291460
  12.5 61.2 %collective-permute-start.3 = (bf16[64,64,128]{2,1,0:T(8,128)(2,1)}, bf16[64,64,128]{2,1,0:T(8,128)(2,1)}, u32[]{:S(2)}, u32[]{:S(2)}) collective-permute-start(bf16[64,64,128]{2,1,0:T(8,128)(2,1)} %get-tuple-element.69), channel_id=1, source_target_pairs={{0,16},{16,32},{32,48},{48,0},{64,80},{80,96},{96,112},{112,64},{1... | collective-permute-start | bytes 3145736 | tf_op jit(solution)/shard_map/ppermute | solution.py:126
  13.5 79.1 %collective-permute-start.7 = (bf16[32,64,128]{2,1,0:T(8,128)(2,1)}, bf16[32,64,128]{2,1,0:T(8,128)(2,1)}, u32[]{:S(2)}, u32[]{:S(2)}) collective-permute-start(bf16[32,64,128]{2,1,0:T(8,128)(2,1)} %get-tuple-element.75), channel_id=1, source_target_pairs={{0,64},{16,80},{32,96},{48,112},{64,0},{80,16},{96,32},{112,48},{1... | collective-permute-start | bytes 1572872 | tf_op jit(solution)/shard_map/ppermute | solution.py:136
  22.8 14.7 %copy-start.7 = (bf16[32,64,128]{2,1,0:T(8,128)(2,1)S(1)}, bf16[32,64,128]{2,1,0:T(8,128)(2,1)}, u32[]{:S(2)}) copy-start(bf16[32,64,128]{2,1,0:T(8,128)(2,1)} %get-tuple-element.71) | copy-start | bytes 1572868
  22.8 52.8 %all-to-all-start = ((bf16[8,528,128]{2,1,0:T(8,128)(2,1)}), bf16[8,528,128]{2,1,0:T(8,128)(2,1)S(1)}, u32[]{:S(2)}, u32[]{:S(2)}) async-start(bf16[8,528,128]{2,1,0:T(8,128)(2,1)} %attend.1), calls=%async_computation | async-start | bytes 2162688 | tf_op jit(solution)/shard_map/all_to_all | solution.py:412
  31.1 24.8 %copy-start.6 = (bf16[32,64,128]{2,1,0:T(8,128)(2,1)S(1)}, bf16[32,64,128]{2,1,0:T(8,128)(2,1)}, u32[]{:S(2)}) copy-start(bf16[32,64,128]{2,1,0:T(8,128)(2,1)} %get-tuple-element.76) | copy-start | bytes 1572868
  31.1 38.5 %collective-permute-start.12 = (bf16[32,64,128]{2,1,0:T(8,128)(2,1)}, bf16[32,64,128]{2,1,0:T(8,128)(2,1)S(1)}, u32[]{:S(2)}, u32[]{:S(2)}) collective-permute-start(bf16[32,64,128]{2,1,0:T(8,128)(2,1)} %get-tuple-element.81), channel_id=1, source_target_pairs={{0,64},{16,80},{32,96},{48,112},{64,0},{80,16},{96,32},{112,48},{1... | collective-permute-start | bytes 1572872 | tf_op jit(solution)/shard_map/ppermute | solution.py:136
  35.9 34.9 %copy-start.5 = (bf16[32,64,128]{2,1,0:T(8,128)(2,1)S(1)}, bf16[32,64,128]{2,1,0:T(8,128)(2,1)}, u32[]{:S(2)}) copy-start(bf16[32,64,128]{2,1,0:T(8,128)(2,1)} %get-tuple-element.80) | copy-start | bytes 1572868
  36.0 19.5 %collective-permute-start.10 = (bf16[16,64,128]{2,1,0:T(8,128)(2,1)S(1)}, bf16[16,64,128]{2,1,0:T(8,128)(2,1)S(1)}, u32[]{:S(2)}, u32[]{:S(2)}) collective-permute-start(bf16[16,64,128]{2,1,0:T(8,128)(2,1)S(1)} %get-tuple-element.86), channel_id=1, source_target_pairs={{0,16},{16,32},{32,48},{48,0},{64,80},{80,96},{96,112},{112,64},{1... | collective-permute-start | bytes 786440 | tf_op jit(solution)/shard_map/ppermute | solution.py:126
  37.5 36.2 %copy-start.4 = (bf16[32,64,128]{2,1,0:T(8,128)(2,1)S(1)}, bf16[32,64,128]{2,1,0:T(8,128)(2,1)}, u32[]{:S(2)}) copy-start(bf16[32,64,128]{2,1,0:T(8,128)(2,1)} %get-tuple-element.68) | copy-start | bytes 1572868
  37.6 33.2 %collective-permute-start.13 = (bf16[16,64,128]{2,1,0:T(8,128)(2,1)S(1)}, bf16[16,64,128]{2,1,0:T(8,128)(2,1)S(1)}, u32[]{:S(2)}, u32[]{:S(2)}) collective-permute-start(bf16[16,64,128]{2,1,0:T(8,128)(2,1)S(1)} %get-tuple-element.87), channel_id=1, source_target_pairs={{16,0},{32,16},{48,32},{0,48},{80,64},{96,80},{112,96},{64,112},{1... | collective-permute-start | bytes 786440 | tf_op jit(solution)/shard_map/ppermute | solution.py:132
  55.5 20.2 %collective-permute-start.5 = (bf16[32,64,128]{2,1,0:T(8,128)(2,1)S(1)}, bf16[32,64,128]{2,1,0:T(8,128)(2,1)}, u32[]{:S(2)}, u32[]{:S(2)}) collective-permute-start(bf16[32,64,128]{2,1,0:T(8,128)(2,1)S(1)} %slice_add_fusion), channel_id=1, source_target_pairs={{16,0},{32,16},{48,32},{0,48},{80,64},{96,80},{112,96},{64,112},{1... | collective-permute-start | bytes 1572872 | tf_op jit(solution)/shard_map/ppermute | solution.py:132
  69.6 23.0 %collective-permute-start.11 = (bf16[32,64,128]{2,1,0:T(8,128)(2,1)}, bf16[32,64,128]{2,1,0:T(8,128)(2,1)}, u32[]{:S(2)}, u32[]{:S(2)}) collective-permute-start(bf16[32,64,128]{2,1,0:T(8,128)(2,1)} %pad_add_fusion.1), channel_id=1, source_target_pairs={{0,16},{16,32},{32,48},{48,0},{64,80},{80,96},{96,112},{112,64},{1... | collective-permute-start | bytes 1572872 | tf_op jit(solution)/shard_map/ppermute | solution.py:126
  71.7 20.9 %collective-permute-start.14 = (bf16[32,64,128]{2,1,0:T(8,128)(2,1)}, bf16[32,64,128]{2,1,0:T(8,128)(2,1)}, u32[]{:S(2)}, u32[]{:S(2)}) collective-permute-start(bf16[32,64,128]{2,1,0:T(8,128)(2,1)} %pad_add_fusion), channel_id=1, source_target_pairs={{16,0},{32,16},{48,32},{0,48},{80,64},{96,80},{112,96},{64,112},{1... | collective-permute-start | bytes 1572872 | tf_op jit(solution)/shard_map/ppermute | solution.py:132
  75.6 27.1 %collective-permute-start.4 = (bf16[32,64,128]{2,1,0:T(8,128)(2,1)}, bf16[32,64,128]{2,1,0:T(8,128)(2,1)}, u32[]{:S(2)}, u32[]{:S(2)}) collective-permute-start(bf16[32,64,128]{2,1,0:T(8,128)(2,1)} %slice_add_fusion.1), channel_id=1, source_target_pairs={{0,16},{16,32},{32,48},{48,0},{64,80},{80,96},{96,112},{112,64},{1... | collective-permute-start | bytes 1572872 | tf_op jit(solution)/shard_map/ppermute | solution.py:126
  75.6 1.0 copy-start
  80.2 12.4 %copy-start.3 = (bf16[32,64,128]{2,1,0:T(8,128)(2,1)S(1)}, bf16[32,64,128]{2,1,0:T(8,128)(2,1)}, u32[]{:S(2)}) copy-start(bf16[32,64,128]{2,1,0:T(8,128)(2,1)} %get-tuple-element.74) | copy-start | bytes 1572868
  80.2 33.8 %all-to-all-start.1 = ((bf16[8,8,16,512]{3,2,1,0:T(8,128)(2,1)}), bf16[8,8,16,512]{3,2,1,0:T(8,128)(2,1)S(1)}, u32[]{:S(2)}, u32[]{:S(2)}) async-start(bf16[8,8,16,512]{3,2,1,0:T(8,128)(2,1)} %join.1), calls=%async_computation.1 | async-start | bytes 2097152 | tf_op jit(solution)/shard_map/all_to_all | solution.py:412
  87.5 24.6 %copy-start.2 = (bf16[32,64,128]{2,1,0:T(8,128)(2,1)S(1)}, bf16[32,64,128]{2,1,0:T(8,128)(2,1)}, u32[]{:S(2)}) copy-start(bf16[32,64,128]{2,1,0:T(8,128)(2,1)} %get-tuple-element.66) | copy-start | bytes 1572868
  89.0 23.1 %collective-permute-start.6 = (bf16[32,64,128]{2,1,0:T(8,128)(2,1)S(1)}, bf16[32,64,128]{2,1,0:T(8,128)(2,1)S(1)}, u32[]{:S(2)}, u32[]{:S(2)}) collective-permute-start(bf16[32,64,128]{2,1,0:T(8,128)(2,1)S(1)} %add_add_fusion), channel_id=1, source_target_pairs={{0,64},{16,80},{32,96},{48,112},{64,0},{80,16},{96,32},{112,48},{1... | collective-permute-start | bytes 1572872 | tf_op jit(solution)/shard_map/ppermute | solution.py:136
where the time goes:
time: 116 us; the launch traced here: 115 us
  waiting for transfers between devices  44.7 us (39%)
  starting transfers between devices  41.7 us (36%)
  Pallas kernels  13.6 us (12%)
  other arithmetic  12.2 us (11%)
  local copies, waits for them, and re-layouts  2.01 us (2%)
    ppermute x4, waiting for transfers between devices, right(): return lax.ppermute(x, 'inst', route)  23.6 us
    ppermute x5, waiting for transfers between devices, across(): lax.ppermute(x, 'inst', [(i, i ^ COLS) for i in range(lax.axis_size('inst...  21.1 us
    all_to_all x2, starting transfers between devices, spread(): return lax.all_to_all(x, 'inst', split_axis=0, concat_axis=0, tiled=True)  15.5 us
    ppermute x5, starting transfers between devices, across(): lax.ppermute(x, 'inst', [(i, i ^ COLS) for i in range(lax.axis_size('inst...  14.2 us
    ppermute x4, starting transfers between devices, left(): return lax.ppermute(x, 'inst', route)  7.66 us
    pallas_call x1, Pallas kernels, attend(): pl.pallas_call(attend_body, in_specs=[smem] * 3 + [anyspace] * 7, out_spe...  5.87 us
    pallas_call x1, Pallas kernels, pack(): pl.pallas_call(functools.partial(pack_body, groups_k, groups_v), in_specs...  4.24 us
    unnamed x2, other arithmetic  4.19 us
  transfers between devices with their start and end apart: 17, of which 4 were waited for; matrix products, arithmetic and copies ran while one was open for 11% of the time, Pallas kernels for 12%

commit v1 on v0

--- a/solution.py
+++ b/solution.py
@@ -361,9 +361,8 @@
     load = pltpu.make_async_copy(arrived, got, sem)
     load.start()
     insts, _, head_dim = got.shape
-    rows = out.shape[1]
-    draft = out.shape[2]
-    heads = out.shape[3] // head_dim
+    rows, draft, width = out.shape
+    heads = width // head_dim
     qrows = draft * heads
     fold = head_dim // heads
     lane = lax.broadcasted_iota(jnp.int32, (draft, head_dim), 1)
@@ -390,22 +389,57 @@
             total = total + share
             acc = acc + share * got[s, a * qrows : (a + 1) * qrows, :].astype(jnp.float32)
         res = (acc / total).astype(out.dtype)
-        for d in range(insts):
-            for h in range(heads):
-                out[d, a, :, h * head_dim : (h + 1) * head_dim] = res[h * draft : (h + 1) * draft]
+        for h in range(heads):
+            out[a, :, h * head_dim : (h + 1) * head_dim] = res[h * draft : (h + 1) * draft]
 
 
 def join(got, rows, draft, width):
-    insts = got.shape[0]
     vmem = pl.BlockSpec(memory_space=pltpu.VMEM)
     return pl.pallas_call(
         join_body,
         in_specs=[pl.BlockSpec(memory_space=pl.ANY)],
         out_specs=vmem,
-        out_shape=jax.ShapeDtypeStruct((insts, rows, draft, width), got.dtype),
+        out_shape=jax.ShapeDtypeStruct((rows, draft, width), got.dtype),
         scratch_shapes=[pltpu.VMEM(got.shape, got.dtype), pltpu.SemaphoreType.DMA],
         name="join",
     )(got)
+
+
+def place_body(per, table, pair, east, far_own, far_other, west, out, sems):
+    rows = far_own.shape[0]
+    pieces = (
+        pair.at[:rows], pair.at[rows:], east.at[:rows], east.at[rows:],
+        far_own, far_other, west.at[:rows], west.at[rows:],
+    )
+    copies = [
+        pltpu.make_async_copy(
+            piece, out.at[pl.ds(table[p] // per * rows, rows)], sems.at[p]
+        )
+        for p, piece in enumerate(pieces)
+    ]
+    for copy in copies:
+        copy.start()
+    for copy in copies:
+        copy.wait()
+
+
+def results(mine, table, per, shape):
+    rows = mine.shape[0]
+    other = across(mine)
+    pair = jnp.concatenate([mine, other])
+    west = right(pair)
+    east = left(pair)
+    far_own = right(west[:rows])
+    far_other = left(east[rows:])
+    vmem = pl.BlockSpec(memory_space=pltpu.VMEM)
+    return pl.pallas_call(
+        functools.partial(place_body, per),
+        in_specs=[pl.BlockSpec(memory_space=pltpu.SMEM)] + [vmem] * 5,
+        out_specs=pl.BlockSpec(memory_space=pl.ANY),
+        out_shape=jax.ShapeDtypeStruct(shape, mine.dtype),
+        scratch_shapes=[pltpu.SemaphoreType.DMA((8,))],
+        name="place",
+    )(table, pair, east, far_own, far_other, west)
 
 
 def spread(x):
@@ -448,7 +482,7 @@
     moved_values = move_values(far2, far1, far3, near, rest_v).reshape(shape)
     got = spread(packet)
     mine = join(got, rows, queries.shape[1], queries.shape[2])
-    attended = spread(mine).reshape(queries.shape)
+    attended = results(mine, table, blocks // insts, queries.shape)
     return moved_keys, moved_values, attended
 
 

time: 116 us -> 111 us (0.957)
  waiting for transfers between devices: 44.7 us -> 35.6 us
  starting transfers between devices: 41.7 us -> 44 us
  Pallas kernels: 13.6 us -> 15.5 us
    ppermute x5 -> x6, waiting for transfers between devices: 21.1 us -> 13.8 us  [across(): lax.ppermute(x, 'inst', [(i, i ^ COLS) for i in range(lax.axis_size('inst...]
    all_to_all x2 -> x1, starting transfers between devices: 15.5 us -> 8.24 us  [spread(): return lax.all_to_all(x, 'inst', split_axis=0, concat_axis=0, tiled=True)]
    ppermute x4 -> x6, starting transfers between devices: 7.66 us -> 13.9 us  [left(): return lax.ppermute(x, 'inst', route)]
    ppermute x5 -> x6, starting transfers between devices: 14.2 us -> 17.1 us  [across(): lax.ppermute(x, 'inst', [(i, i ^ COLS) for i in range(lax.axis_size('inst...]
    pallas_call x0 -> x1, Pallas kernels: none -> 2.25 us  [results(): pl.pallas_call(functools.partial(place_body, per), in_specs=[pl.BlockSpec...]
    ppermute x4 -> x6, waiting for transfers between devices: 23.6 us -> 21.8 us  [right(): return lax.ppermute(x, 'inst', route)]
    ppermute x4 -> x6, starting transfers between devices: 3.72 us -> 4.2 us  [right(): return lax.ppermute(x, 'inst', route)]
  transfers between devices with their start and end apart: 17 -> 21, of which waited for: 4 -> 5; matrix products, arithmetic and copies ran while one was open for 11% -> 11% of each run, Pallas kernels for 12% -> 12%
where the time goes in v1:
time: 111 us; the launch traced here: 110 us
  starting transfers between devices  44 us (40%)
  waiting for transfers between devices  35.6 us (32%)
  Pallas kernels  15.5 us (14%)
  other arithmetic  12.1 us (11%)
  local copies, waits for them, and re-layouts  2.32 us (2%)
    ppermute x6, waiting for transfers between devices, right(): return lax.ppermute(x, 'inst', route)  21.8 us
    ppermute x6, starting transfers between devices, across(): lax.ppermute(x, 'inst', [(i, i ^ COLS) for i in range(lax.axis_size('inst...  17.1 us
    ppermute x6, starting transfers between devices, left(): return lax.ppermute(x, 'inst', route)  13.9 us
    ppermute x6, waiting for transfers between devices, across(): lax.ppermute(x, 'inst', [(i, i ^ COLS) for i in range(lax.axis_size('inst...  13.8 us
    all_to_all x1, starting transfers between devices, spread(): return lax.all_to_all(x, 'inst', split_axis=0, concat_axis=0, tiled=True)  8.24 us
    pallas_call x1, Pallas kernels, attend(): pl.pallas_call(attend_body, in_specs=[smem] * 3 + [anyspace] * 7, out_spe...  5.88 us
    pallas_call x1, Pallas kernels, pack(): pl.pallas_call(functools.partial(pack_body, groups_k, groups_v), in_specs...  4.22 us
    ppermute x6, starting transfers between devices, right(): return lax.ppermute(x, 'inst', route)  4.2 us
  transfers between devices with their start and end apart: 21, of which 5 were waited for; matrix products, arithmetic and copies ran while one was open for 11% of the time, Pallas kernels for 12%

profile of v1, /device:TPU:0, one launch (start us, length us, event | category | flops | bytes accessed | tf_op | source)
XLA Modules:
  0.0 110.5 jit_solution(3730102770831593510)
XLA Ops:
  0.6 0.1 collective-permute-start
  0.7 0.5 collective-permute-start.1
  1.2 0.6 compare_select_fusion.4.base.meta.table
  1.8 4.2 %shard_map.103 = (bf16[64,64,128]{2,1,0:T(8,128)(2,1)}, bf16[64,64,128]{2,1,0:T(8,128)(2,1)}, bf16[32,64,128]{2,1,0:T(8,128)(2,1)}, bf16[32,64,128]{2,1,0:T(8,12...) custom-call(s32[128]{0:T(128)} %old_block.3, ...), custom_call_target="tpu_custom_call" | custom-call | tf_op jit(solution)/shard_map/pallas_call | solution.py:104
  6.0 2.9 %collective-permute-start.2 = (bf16[64,64,128]{2,1,0:T(8,128)(2,1)}, bf16[64,64,128]{2,1,0:T(8,128)(2,1)S(1)}, u32[]{:S(2)}, u32[]{:S(2)}) collective-permute-start(bf16[64,64,128]{2,1,0:T(8,128)(2,1)} %get-tuple-element.67), channel_id=1, source_target_pairs={{16,0},{32,16},{48,32},{0,48},{80,64},{96,80},{112,96},{64,112},{1... | collective-permute-start | bytes 3145736 | tf_op jit(solution)/shard_map/ppermute | solution.py:132
  8.9 3.2 %collective-permute-start.9 = (bf16[32,64,128]{2,1,0:T(8,128)(2,1)}, bf16[32,64,128]{2,1,0:T(8,128)(2,1)}, u32[]{:S(2)}, u32[]{:S(2)}) collective-permute-start(bf16[32,64,128]{2,1,0:T(8,128)(2,1)} %get-tuple-element.79), channel_id=1, source_target_pairs={{0,64},{16,80},{32,96},{48,112},{64,0},{80,16},{96,32},{112,48},{1... | collective-permute-start | bytes 1572872 | tf_op jit(solution)/shard_map/ppermute | solution.py:136
  12.1 0.3 collective-permute-start.8
  12.5 0.0 collective-permute-done.ok
  12.5 1.0 collective-permute-start.3
  13.5 3.5 %collective-permute-start.7 = (bf16[32,64,128]{2,1,0:T(8,128)(2,1)}, bf16[32,64,128]{2,1,0:T(8,128)(2,1)}, u32[]{:S(2)}, u32[]{:S(2)}) collective-permute-start(bf16[32,64,128]{2,1,0:T(8,128)(2,1)} %get-tuple-element.75), channel_id=1, source_target_pairs={{0,64},{16,80},{32,96},{48,112},{64,0},{80,16},{96,32},{112,48},{1... | collective-permute-start | bytes 1572872 | tf_op jit(solution)/shard_map/ppermute | solution.py:136
  17.0 5.9 %attend.1 = bf16[8,528,128]{2,1,0:T(8,128)(2,1)} custom-call(s32[128]{0:T(128)} %old_block.3, s32[64]{0:T(128)} %lengths.1, s32[16]{0:T(128)} %compare_select_fusion.4.base.meta.table, bf16[64,16,512]{2,1,0:T(8,128)(2,1)} %q, bf16[128,64,128]{2,1,0:T(8,128)(2,1)} %bitcast.12, bf16[128,64,128]{2,1,0:T(8,128)(2,1)} %bitcast.15, ...), custom_call_target="tpu_custom_call" | custom-call | tf_op jit(solution)/shard_map/attend/pallas_call | solution.py:335
  22.8 0.0 copy-start.10
  22.9 8.2 %all-to-all-start = ((bf16[8,528,128]{2,1,0:T(8,128)(2,1)}), bf16[8,528,128]{2,1,0:T(8,128)(2,1)S(1)}, u32[]{:S(2)}, u32[]{:S(2)}) async-start(bf16[8,528,128]{2,1,0:T(8,128)(2,1)} %attend.1), calls=%async_computation | async-start | bytes 2162688 | tf_op jit(solution)/shard_map/all_to_all | solution.py:446
  31.1 3.6 %collective-permute-start.12 = (bf16[32,64,128]{2,1,0:T(8,128)(2,1)}, bf16[32,64,128]{2,1,0:T(8,128)(2,1)S(1)}, u32[]{:S(2)}, u32[]{:S(2)}) collective-permute-start(bf16[32,64,128]{2,1,0:T(8,128)(2,1)} %get-tuple-element.81), channel_id=1, source_target_pairs={{0,64},{16,80},{32,96},{48,112},{64,0},{80,16},{96,32},{112,48},{1... | collective-permute-start | bytes 1572872 | tf_op jit(solution)/shard_map/ppermute | solution.py:136
  34.7 1.2 %slice_add_fusion.4 = (bf16[16,64,128]{2,1,0:T(8,128)(2,1)S(1)}, bf16[16,64,128]{2,1,0:T(8,128)(2,1)S(1)}) fusion(bf16[32,64,128]{2,1,0:T(8,128)(2,1)} %collective-permute-done.9, bf16[32,64,128]{2,1,0:T(8,128)(2,1)} %get-tuple-element.78), kind=kLoop, calls=%fused_computation.11 | loop fusion | flops 262144 | bytes 1572864 | tf_op jit(solution)/shard_map/add | solution.py:153
  36.0 0.0 collective-permute-done.2
  36.0 1.5 %collective-permute-start.10 = (bf16[16,64,128]{2,1,0:T(8,128)(2,1)S(1)}, bf16[16,64,128]{2,1,0:T(8,128)(2,1)S(1)}, u32[]{:S(2)}, u32[]{:S(2)}) collective-permute-start(bf16[16,64,128]{2,1,0:T(8,128)(2,1)S(1)} %get-tuple-element.86), channel_id=1, source_target_pairs={{0,16},{16,32},{32,48},{48,0},{64,80},{80,96},{96,112},{112,64},{1... | collective-permute-start | bytes 786440 | tf_op jit(solution)/shard_map/ppermute | solution.py:126
  37.5 0.1 slice_add_fusion
  37.6 0.0 copy-start.7
  37.6 2.2 %collective-permute-start.13 = (bf16[16,64,128]{2,1,0:T(8,128)(2,1)S(1)}, bf16[16,64,128]{2,1,0:T(8,128)(2,1)S(1)}, u32[]{:S(2)}, u32[]{:S(2)}) collective-permute-start(bf16[16,64,128]{2,1,0:T(8,128)(2,1)S(1)} %get-tuple-element.87), channel_id=1, source_target_pairs={{16,0},{32,16},{48,32},{0,48},{80,64},{96,80},{112,96},{64,112},{1... | collective-permute-start | bytes 786440 | tf_op jit(solution)/shard_map/ppermute | solution.py:132
  39.8 15.6 %collective-permute-done.10 = bf16[16,64,128]{2,1,0:T(8,128)(2,1)S(1)} collective-permute-done((bf16[16,64,128]{2,1,0:T(8,128)(2,1)S(1)}, bf16[16,64,128]{2,1,0:T(8,128)(2,1)S(1)}, u32[]{:S(2)}, u32[]{:S(2)}) %collective-permute-start.10) | collective-permute-done | bytes 262176 | tf_op jit(solution)/shard_map/ppermute | solution.py:126
  55.4 0.4 collective-permute-start.5
  55.9 1.9 %pad_add_fusion.1 = bf16[32,64,128]{2,1,0:T(8,128)(2,1)} fusion(bf16[16,64,128]{2,1,0:T(8,128)(2,1)S(1)} %collective-permute-done.10, bf16[32,64,128]{2,1,0:T(8,128)(2,1)S(1)} %copy-done.9, bf16[32,64,128]{2,1,0:T(8,128)(2,1)} %collective-permute-done.8), kind=kLoop, calls=%fused_computation.8 | loop fusion | flops 524288 | bytes 1835008 | tf_op jit(solution)/shard_map/add | solution.py:156
  57.8 11.8 %collective-permute-done.12 = bf16[32,64,128]{2,1,0:T(8,128)(2,1)S(1)} collective-permute-done((bf16[32,64,128]{2,1,0:T(8,128)(2,1)}, bf16[32,64,128]{2,1,0:T(8,128)(2,1)S(1)}, u32[]{:S(2)}, u32[]{:S(2)}) %collective-permute-start.12) | collective-permute-done | bytes 524320 | tf_op jit(solution)/shard_map/ppermute | solution.py:136
  69.6 1.2 %collective-permute-start.11 = (bf16[32,64,128]{2,1,0:T(8,128)(2,1)}, bf16[32,64,128]{2,1,0:T(8,128)(2,1)}, u32[]{:S(2)}, u32[]{:S(2)}) collective-permute-start(bf16[32,64,128]{2,1,0:T(8,128)(2,1)} %pad_add_fusion.1), channel_id=1, source_target_pairs={{0,16},{16,32},{32,48},{48,0},{64,80},{80,96},{96,112},{112,64},{1... | collective-permute-start | bytes 1572872 | tf_op jit(solution)/shard_map/ppermute | solution.py:126
  70.8 0.9 pad_add_fusion
  71.7 2.0 %collective-permute-start.14 = (bf16[32,64,128]{2,1,0:T(8,128)(2,1)}, bf16[32,64,128]{2,1,0:T(8,128)(2,1)}, u32[]{:S(2)}, u32[]{:S(2)}) collective-permute-start(bf16[32,64,128]{2,1,0:T(8,128)(2,1)} %pad_add_fusion), channel_id=1, source_target_pairs={{16,0},{32,16},{48,32},{0,48},{80,64},{96,80},{112,96},{64,112},{1... | collective-permute-start | bytes 1572872 | tf_op jit(solution)/shard_map/ppermute | solution.py:132
  73.7 0.0 collective-permute-done.3
  73.7 1.9 %slice_add_fusion.1 = bf16[32,64,128]{2,1,0:T(8,128)(2,1)} fusion(bf16[32,64,128]{2,1,0:T(8,128)(2,1)S(1)} %copy-done.7, bf16[64,64,128]{2,1,0:T(8,128)(2,1)} %collective-permute-done.3), kind=kLoop, calls=%fused_computation.1 | loop fusion | flops 262144 | bytes 1572864 | tf_op jit(solution)/shard_map/add | solution.py:142
  75.6 0.0 collective-permute-start.4
  75.6 1.0 copy-done
  76.6 3.2 %join.1 = bf16[8,16,512]{2,1,0:T(8,128)(2,1)} custom-call(bf16[8,528,128]{2,1,0:T(8,128)(2,1)} %copy-done), custom_call_target="tpu_custom_call" | custom-call | tf_op jit(solution)/shard_map/join/pallas_call | solution.py:398
  79.8 0.0 copy-start.11
  79.8 3.3 %collective-permute-start.15 = (bf16[8,16,512]{2,1,0:T(8,128)(2,1)}, bf16[8,16,512]{2,1,0:T(8,128)(2,1)S(1)}, u32[]{:S(2)}, u32[]{:S(2)}) collective-permute-start(bf16[8,16,512]{2,1,0:T(8,128)(2,1)} %join.1), channel_id=1, source_target_pairs={{0,64},{16,80},{32,96},{48,112},{64,0},{80,16},{96,32},{112,48},{1... | collective-permute-start | bytes 393224 | tf_op jit(solution)/shard_map/ppermute | solution.py:136
  83.1 1.4 %add_add_fusion = bf16[32,64,128]{2,1,0:T(8,128)(2,1)S(1)} fusion(bf16[32,64,128]{2,1,0:T(8,128)(2,1)} %collective-permute-done.5, bf16[32,64,128]{2,1,0:T(8,128)(2,1)} %get-tuple-element.70, bf16[64,64,128]{2,1,0:T(8,128)(2,1)} %collective-permute-done.3), kind=kLoop, calls=%fused_computation.9 | loop fusion | flops 524288 | bytes 2097152 | tf_op jit(solution)/shard_map/add | solution.py:145
  84.6 2.0 %collective-permute-done.15 = bf16[8,16,512]{2,1,0:T(8,128)(2,1)S(1)} collective-permute-done((bf16[8,16,512]{2,1,0:T(8,128)(2,1)}, bf16[8,16,512]{2,1,0:T(8,128)(2,1)S(1)}, u32[]{:S(2)}, u32[]{:S(2)}) %collective-permute-start.15) | collective-permute-done | bytes 131104 | tf_op jit(solution)/shard_map/ppermute | solution.py:136
  86.6 3.2 %collective-permute-start.6 = (bf16[32,64,128]{2,1,0:T(8,128)(2,1)S(1)}, bf16[32,64,128]{2,1,0:T(8,128)(2,1)S(1)}, u32[]{:S(2)}, u32[]{:S(2)}) collective-permute-start(bf16[32,64,128]{2,1,0:T(8,128)(2,1)S(1)} %add_add_fusion), channel_id=1, source_target_pairs={{0,64},{16,80},{32,96},{48,112},{64,0},{80,16},{96,32},{112,48},{1... | collective-permute-start | bytes 1572872 | tf_op jit(solution)/shard_map/ppermute | solution.py:136
  89.9 0.1 collective-permute-start.17
  90.0 3.2 %collective-permute-start.16 = (bf16[16,16,512]{2,1,0:T(8,128)(2,1)S(1)}, bf16[16,16,512]{2,1,0:T(8,128)(2,1)S(1)}, u32[]{:S(2)}, u32[]{:S(2)}) collective-permute-start(bf16[16,16,512]{2,1,0:T(8,128)(2,1)S(1)} %pad_maximum_fusion.pair), channel_id=1, source_target_pairs={{16,0},{32,16},{48,32},{0,48},{80,64},{96,80},{112,96},{64,112},{1... | collective-permute-start | bytes 786440 | tf_op jit(solution)/shard_map/ppermute | solution.py:132
  93.2 2.3 %add_bitcast_fusion = bf16[32,1,64,128]{3,2,1,0:T(8,128)(2,1)} fusion(bf16[32,64,128]{2,1,0:T(8,128)(2,1)} %collective-permute-done.14, bf16[32,64,128]{2,1,0:T(8,128)(2,1)} %collective-permute-done.11, bf16[32,64,128]{2,1,0:T(8,128)(2,1)S(1)} %copy-done.6, bf16[32,64,128]{2,1,0:T(8,128)(2,1)} %collective-permute-done.7), kind=kLoop, calls=%fused_computation.6 | loop fusion | flops 786432 | bytes 2621440
  95.5 5.2 %collective-permute-done.17.west = bf16[16,16,512]{2,1,0:T(8,128)(2,1)S(1)} collective-permute-done((bf16[16,16,512]{2,1,0:T(8,128)(2,1)S(1)}, bf16[16,16,512]{2,1,0:T(8,128)(2,1)S(1)}, u32[]{:S(2)}, u32[]{:S(2)}) %collective-permute-start.17) | collective-permute-done | bytes 262176 | tf_op jit(solution)/shard_map/ppermute | solution.py:126
  100.7 0.4 collective-permute-start.18
  101.0 3.0 %collective-permute-start.19 = (bf16[8,16,512]{2,1,0:T(8,128)(2,1)S(1)}, bf16[8,16,512]{2,1,0:T(8,128)(2,1)S(1)}, u32[]{:S(2)}, u32[]{:S(2)}) collective-permute-start(bf16[8,16,512]{2,1,0:T(8,128)(2,1)S(1)} %slice.46), channel_id=1, source_target_pairs={{16,0},{32,16},{48,32},{0,48},{80,64},{96,80},{112,96},{64,112},{1... | collective-permute-start | bytes 393224 | tf_op jit(solution)/shard_map/ppermute | solution.py:132
  104.1 1.9 %fusion.2 = bf16[32,1,64,128]{3,2,1,0:T(8,128)(2,1)} fusion(bf16[32,64,128]{2,1,0:T(8,128)(2,1)S(1)} %collective-permute-done.6, bf16[32,64,128]{2,1,0:T(8,128)(2,1)} %collective-permute-done.4, bf16[32,64,128]{2,1,0:T(8,128)(2,1)S(1)} %copy-done.5, bf16[64,64,128]{2,1,0:T(8,128)(2,1)S(1)} %collective-permute-done.2), kind=kLoop, calls=%fused_computation.5 | loop fusion | flops 786432 | bytes 2621440
  106.0 0.9 collective-permute-done.18.far_own
  106.9 0.6 copy-done.12
  107.6 0.6 copy-done.13
  108.2 2.3 %place.1 = bf16[64,16,512]{2,1,0:T(8,128)(2,1)} custom-call(s32[16]{0:T(128)} %compare_select_fusion.4.base.meta.table, bf16[16,16,512]{2,1,0:T(8,128)(2,1)} %copy-done.2, bf16[16,16,512]{2,1,0:T(8,128)(2,1)} %copy-done.4, bf16[8,16,512]{2,1,0:T(8,128)(2,1)} %copy-done.12, bf16[8,16,512]{2,1,0:T(8,128)(2,1)} %copy-done.13, bf16[16,16,512]{2,1,0:T(8,128)(2,1)} %copy-done.3), custom_call_target="tpu_custom_call" | custom-call | tf_op jit(solution)/shard_map/place/pallas_call | solution.py:435
  (38 shorter events, 0.1 us)
Async XLA Ops:
  0.6 11.8 %collective-permute-start = (bf16[128,64,128]{2,1,0:T(8,128)(2,1)}, bf16[128,64,128]{2,1,0:T(8,128)(2,1)S(1)}, u32[]{:S(2)}, u32[]{:S(2)}) collective-permute-start(bf16[128,64,128]{2,1,0:T(8,128)(2,1)} %bitcast.10), channel_id=1, source_target_pairs={{0,1},{1,0},{2,3},{3,2},{4,5},{5,4},{6,7},{7,6},{8,9},{9,8},{10,11... | collective-permute-start | bytes 6291464 | tf_op jit(solution)/shard_map/ppermute | solution.py:460
  0.7 12.8 %collective-permute-start.1 = (bf16[128,64,128]{2,1,0:T(8,128)(2,1)}, bf16[128,64,128]{2,1,0:T(8,128)(2,1)}, u32[]{:S(2)}, u32[]{:S(2)}) collective-permute-start(bf16[128,64,128]{2,1,0:T(8,128)(2,1)} %bitcast.13), channel_id=1, source_target_pairs={{0,1},{1,0},{2,3},{3,2},{4,5},{5,4},{6,7},{7,6},{8,9},{9,8},{10,11... | collective-permute-start | bytes 6291464 | tf_op jit(solution)/shard_map/ppermute | solution.py:461
  6.0 30.0 %collective-permute-start.2 = (bf16[64,64,128]{2,1,0:T(8,128)(2,1)}, bf16[64,64,128]{2,1,0:T(8,128)(2,1)S(1)}, u32[]{:S(2)}, u32[]{:S(2)}) collective-permute-start(bf16[64,64,128]{2,1,0:T(8,128)(2,1)} %get-tuple-element.67), channel_id=1, source_target_pairs={{16,0},{32,16},{48,32},{0,48},{80,64},{96,80},{112,96},{64,112},{1... | collective-permute-start | bytes 3145736 | tf_op jit(solution)/shard_map/ppermute | solution.py:132
  8.9 22.2 %collective-permute-start.9 = (bf16[32,64,128]{2,1,0:T(8,128)(2,1)}, bf16[32,64,128]{2,1,0:T(8,128)(2,1)}, u32[]{:S(2)}, u32[]{:S(2)}) collective-permute-start(bf16[32,64,128]{2,1,0:T(8,128)(2,1)} %get-tuple-element.79), channel_id=1, source_target_pairs={{0,64},{16,80},{32,96},{48,112},{64,0},{80,16},{96,32},{112,48},{1... | collective-permute-start | bytes 1572872 | tf_op jit(solution)/shard_map/ppermute | solution.py:136
  12.1 25.4 %collective-permute-start.8 = (bf16[32,64,128]{2,1,0:T(8,128)(2,1)}, bf16[32,64,128]{2,1,0:T(8,128)(2,1)}, u32[]{:S(2)}, u32[]{:S(2)}) collective-permute-start(bf16[32,64,128]{2,1,0:T(8,128)(2,1)} %get-tuple-element.77), channel_id=1, source_target_pairs={{0,64},{16,80},{32,96},{48,112},{64,0},{80,16},{96,32},{112,48},{1... | collective-permute-start | bytes 1572872 | tf_op jit(solution)/shard_map/ppermute | solution.py:136
  12.5 4.5 %copy-start.1 = (bf16[128,64,128]{2,1,0:T(8,128)(2,1)}, bf16[128,64,128]{2,1,0:T(8,128)(2,1)S(1)}, u32[]{:S(2)}) copy-start(bf16[128,64,128]{2,1,0:T(8,128)(2,1)S(1)} %collective-permute-done.ok) | copy-start | bytes 6291460
  12.5 61.2 %collective-permute-start.3 = (bf16[64,64,128]{2,1,0:T(8,128)(2,1)}, bf16[64,64,128]{2,1,0:T(8,128)(2,1)}, u32[]{:S(2)}, u32[]{:S(2)}) collective-permute-start(bf16[64,64,128]{2,1,0:T(8,128)(2,1)} %get-tuple-element.69), channel_id=1, source_target_pairs={{0,16},{16,32},{32,48},{48,0},{64,80},{80,96},{96,112},{112,64},{1... | collective-permute-start | bytes 3145736 | tf_op jit(solution)/shard_map/ppermute | solution.py:126
  13.5 76.4 %collective-permute-start.7 = (bf16[32,64,128]{2,1,0:T(8,128)(2,1)}, bf16[32,64,128]{2,1,0:T(8,128)(2,1)}, u32[]{:S(2)}, u32[]{:S(2)}) collective-permute-start(bf16[32,64,128]{2,1,0:T(8,128)(2,1)} %get-tuple-element.75), channel_id=1, source_target_pairs={{0,64},{16,80},{32,96},{48,112},{64,0},{80,16},{96,32},{112,48},{1... | collective-permute-start | bytes 1572872 | tf_op jit(solution)/shard_map/ppermute | solution.py:136
  22.8 14.7 %copy-start.10 = (bf16[32,64,128]{2,1,0:T(8,128)(2,1)S(1)}, bf16[32,64,128]{2,1,0:T(8,128)(2,1)}, u32[]{:S(2)}) copy-start(bf16[32,64,128]{2,1,0:T(8,128)(2,1)} %get-tuple-element.71) | copy-start | bytes 1572868
  22.9 52.7 %all-to-all-start = ((bf16[8,528,128]{2,1,0:T(8,128)(2,1)}), bf16[8,528,128]{2,1,0:T(8,128)(2,1)S(1)}, u32[]{:S(2)}, u32[]{:S(2)}) async-start(bf16[8,528,128]{2,1,0:T(8,128)(2,1)} %attend.1), calls=%async_computation | async-start | bytes 2162688 | tf_op jit(solution)/shard_map/all_to_all | solution.py:446
  31.1 24.8 %copy-start.9 = (bf16[32,64,128]{2,1,0:T(8,128)(2,1)S(1)}, bf16[32,64,128]{2,1,0:T(8,128)(2,1)}, u32[]{:S(2)}) copy-start(bf16[32,64,128]{2,1,0:T(8,128)(2,1)} %get-tuple-element.76) | copy-start | bytes 1572868
  31.1 38.5 %collective-permute-start.12 = (bf16[32,64,128]{2,1,0:T(8,128)(2,1)}, bf16[32,64,128]{2,1,0:T(8,128)(2,1)S(1)}, u32[]{:S(2)}, u32[]{:S(2)}) collective-permute-start(bf16[32,64,128]{2,1,0:T(8,128)(2,1)} %get-tuple-element.81), channel_id=1, source_target_pairs={{0,64},{16,80},{32,96},{48,112},{64,0},{80,16},{96,32},{112,48},{1... | collective-permute-start | bytes 1572872 | tf_op jit(solution)/shard_map/ppermute | solution.py:136
  36.0 34.9 %copy-start.8 = (bf16[32,64,128]{2,1,0:T(8,128)(2,1)S(1)}, bf16[32,64,128]{2,1,0:T(8,128)(2,1)}, u32[]{:S(2)}) copy-start(bf16[32,64,128]{2,1,0:T(8,128)(2,1)} %get-tuple-element.80) | copy-start | bytes 1572868
  36.0 19.5 %collective-permute-start.10 = (bf16[16,64,128]{2,1,0:T(8,128)(2,1)S(1)}, bf16[16,64,128]{2,1,0:T(8,128)(2,1)S(1)}, u32[]{:S(2)}, u32[]{:S(2)}) collective-permute-start(bf16[16,64,128]{2,1,0:T(8,128)(2,1)S(1)} %get-tuple-element.86), channel_id=1, source_target_pairs={{0,16},{16,32},{32,48},{48,0},{64,80},{80,96},{96,112},{112,64},{1... | collective-permute-start | bytes 786440 | tf_op jit(solution)/shard_map/ppermute | solution.py:126
  37.6 36.1 %copy-start.7 = (bf16[32,64,128]{2,1,0:T(8,128)(2,1)S(1)}, bf16[32,64,128]{2,1,0:T(8,128)(2,1)}, u32[]{:S(2)}) copy-start(bf16[32,64,128]{2,1,0:T(8,128)(2,1)} %get-tuple-element.68) | copy-start | bytes 1572868
  37.6 33.2 %collective-permute-start.13 = (bf16[16,64,128]{2,1,0:T(8,128)(2,1)S(1)}, bf16[16,64,128]{2,1,0:T(8,128)(2,1)S(1)}, u32[]{:S(2)}, u32[]{:S(2)}) collective-permute-start(bf16[16,64,128]{2,1,0:T(8,128)(2,1)S(1)} %get-tuple-element.87), channel_id=1, source_target_pairs={{16,0},{32,16},{48,32},{0,48},{80,64},{96,80},{112,96},{64,112},{1... | collective-permute-start | bytes 786440 | tf_op jit(solution)/shard_map/ppermute | solution.py:132
  55.4 20.2 %collective-permute-start.5 = (bf16[32,64,128]{2,1,0:T(8,128)(2,1)S(1)}, bf16[32,64,128]{2,1,0:T(8,128)(2,1)}, u32[]{:S(2)}, u32[]{:S(2)}) collective-permute-start(bf16[32,64,128]{2,1,0:T(8,128)(2,1)S(1)} %slice_add_fusion), channel_id=1, source_target_pairs={{16,0},{32,16},{48,32},{0,48},{80,64},{96,80},{112,96},{64,112},{1... | collective-permute-start | bytes 1572872 | tf_op jit(solution)/shard_map/ppermute | solution.py:132
  69.6 20.3 %collective-permute-start.11 = (bf16[32,64,128]{2,1,0:T(8,128)(2,1)}, bf16[32,64,128]{2,1,0:T(8,128)(2,1)}, u32[]{:S(2)}, u32[]{:S(2)}) collective-permute-start(bf16[32,64,128]{2,1,0:T(8,128)(2,1)} %pad_add_fusion.1), channel_id=1, source_target_pairs={{0,16},{16,32},{32,48},{48,0},{64,80},{80,96},{96,112},{112,64},{1... | collective-permute-start | bytes 1572872 | tf_op jit(solution)/shard_map/ppermute | solution.py:126
  71.7 21.5 %collective-permute-start.14 = (bf16[32,64,128]{2,1,0:T(8,128)(2,1)}, bf16[32,64,128]{2,1,0:T(8,128)(2,1)}, u32[]{:S(2)}, u32[]{:S(2)}) collective-permute-start(bf16[32,64,128]{2,1,0:T(8,128)(2,1)} %pad_add_fusion), channel_id=1, source_target_pairs={{16,0},{32,16},{48,32},{0,48},{80,64},{96,80},{112,96},{64,112},{1... | collective-permute-start | bytes 1572872 | tf_op jit(solution)/shard_map/ppermute | solution.py:132
  75.6 17.6 %copy-start.6 = (bf16[32,64,128]{2,1,0:T(8,128)(2,1)S(1)}, bf16[32,64,128]{2,1,0:T(8,128)(2,1)}, u32[]{:S(2)}) copy-start(bf16[32,64,128]{2,1,0:T(8,128)(2,1)} %get-tuple-element.74) | copy-start | bytes 1572868
  75.6 28.5 %collective-permute-start.4 = (bf16[32,64,128]{2,1,0:T(8,128)(2,1)}, bf16[32,64,128]{2,1,0:T(8,128)(2,1)}, u32[]{:S(2)}, u32[]{:S(2)}) collective-permute-start(bf16[32,64,128]{2,1,0:T(8,128)(2,1)} %slice_add_fusion.1), channel_id=1, source_target_pairs={{0,16},{16,32},{32,48},{48,0},{64,80},{80,96},{96,112},{112,64},{1... | collective-permute-start | bytes 1572872 | tf_op jit(solution)/shard_map/ppermute | solution.py:126
  75.6 1.0 copy-start
  79.8 10.0 %copy-start.11 = (bf16[8,16,512]{2,1,0:T(8,128)(2,1)S(1)}, bf16[8,16,512]{2,1,0:T(8,128)(2,1)}, u32[]{:S(2)}) copy-start(bf16[8,16,512]{2,1,0:T(8,128)(2,1)} %join.1) | copy-start | bytes 393220
  79.8 6.8 %collective-permute-start.15 = (bf16[8,16,512]{2,1,0:T(8,128)(2,1)}, bf16[8,16,512]{2,1,0:T(8,128)(2,1)S(1)}, u32[]{:S(2)}, u32[]{:S(2)}) collective-permute-start(bf16[8,16,512]{2,1,0:T(8,128)(2,1)} %join.1), channel_id=1, source_target_pairs={{0,64},{16,80},{32,96},{48,112},{64,0},{80,16},{96,32},{112,48},{1... | collective-permute-start | bytes 393224 | tf_op jit(solution)/shard_map/ppermute | solution.py:136
  84.6 19.5 %copy-start.5 = (bf16[32,64,128]{2,1,0:T(8,128)(2,1)S(1)}, bf16[32,64,128]{2,1,0:T(8,128)(2,1)}, u32[]{:S(2)}) copy-start(bf16[32,64,128]{2,1,0:T(8,128)(2,1)} %get-tuple-element.66) | copy-start | bytes 1572868
  86.6 17.5 %collective-permute-start.6 = (bf16[32,64,128]{2,1,0:T(8,128)(2,1)S(1)}, bf16[32,64,128]{2,1,0:T(8,128)(2,1)S(1)}, u32[]{:S(2)}, u32[]{:S(2)}) collective-permute-start(bf16[32,64,128]{2,1,0:T(8,128)(2,1)S(1)} %add_add_fusion), channel_id=1, source_target_pairs={{0,64},{16,80},{32,96},{48,112},{64,0},{80,16},{96,32},{112,48},{1... | collective-permute-start | bytes 1572872 | tf_op jit(solution)/shard_map/ppermute | solution.py:136
  89.8 16.2 %copy-start.2 = (bf16[16,16,512]{2,1,0:T(8,128)(2,1)}, bf16[16,16,512]{2,1,0:T(8,128)(2,1)S(1)}, u32[]{:S(2)}) copy-start(bf16[16,16,512]{2,1,0:T(8,128)(2,1)S(1)} %pad_maximum_fusion.pair) | copy-start | bytes 786436
  89.9 10.8 %collective-permute-start.17 = (bf16[16,16,512]{2,1,0:T(8,128)(2,1)S(1)}, bf16[16,16,512]{2,1,0:T(8,128)(2,1)S(1)}, u32[]{:S(2)}, u32[]{:S(2)}) collective-permute-start(bf16[16,16,512]{2,1,0:T(8,128)(2,1)S(1)} %pad_maximum_fusion.pair), channel_id=1, source_target_pairs={{0,16},{16,32},{32,48},{48,0},{64,80},{80,96},{96,112},{112,64},{1... | collective-permute-start | bytes 786440 | tf_op jit(solution)/shard_map/ppermute | solution.py:126
  90.0 11.1 %collective-permute-start.16 = (bf16[16,16,512]{2,1,0:T(8,128)(2,1)S(1)}, bf16[16,16,512]{2,1,0:T(8,128)(2,1)S(1)}, u32[]{:S(2)}, u32[]{:S(2)}) collective-permute-start(bf16[16,16,512]{2,1,0:T(8,128)(2,1)S(1)} %pad_maximum_fusion.pair), channel_id=1, source_target_pairs={{16,0},{32,16},{48,32},{0,48},{80,64},{96,80},{112,96},{64,112},{1... | collective-permute-start | bytes 786440 | tf_op jit(solution)/shard_map/ppermute | solution.py:132
  100.7 6.3 %copy-start.3 = (bf16[16,16,512]{2,1,0:T(8,128)(2,1)}, bf16[16,16,512]{2,1,0:T(8,128)(2,1)S(1)}, u32[]{:S(2)}) copy-start(bf16[16,16,512]{2,1,0:T(8,128)(2,1)S(1)} %collective-permute-done.17.west) | copy-start | bytes 786436
  100.7 6.2 %collective-permute-start.18 = (bf16[8,16,512]{2,1,0:T(8,128)(2,1)S(1)}, bf16[8,16,512]{2,1,0:T(8,128)(2,1)S(1)}, u32[]{:S(2)}, u32[]{:S(2)}) collective-permute-start(bf16[8,16,512]{2,1,0:T(8,128)(2,1)S(1)} %slice.45), channel_id=1, source_target_pairs={{0,16},{16,32},{32,48},{48,0},{64,80},{80,96},{96,112},{112,64},{1... | collective-permute-start | bytes 393224 | tf_op jit(solution)/shard_map/ppermute | solution.py:126
  101.0 5.9 %copy-start.4 = (bf16[16,16,512]{2,1,0:T(8,128)(2,1)}, bf16[16,16,512]{2,1,0:T(8,128)(2,1)S(1)}, u32[]{:S(2)}) copy-start(bf16[16,16,512]{2,1,0:T(8,128)(2,1)S(1)} %collective-permute-done.16.east) | copy-start | bytes 786436
  101.0 5.9 %collective-permute-start.19 = (bf16[8,16,512]{2,1,0:T(8,128)(2,1)S(1)}, bf16[8,16,512]{2,1,0:T(8,128)(2,1)S(1)}, u32[]{:S(2)}, u32[]{:S(2)}) collective-permute-start(bf16[8,16,512]{2,1,0:T(8,128)(2,1)S(1)} %slice.46), channel_id=1, source_target_pairs={{16,0},{32,16},{48,32},{0,48},{80,64},{96,80},{112,96},{64,112},{1... | collective-permute-start | bytes 393224 | tf_op jit(solution)/shard_map/ppermute | solution.py:132
  106.9 0.6 copy-start.12
  107.6 0.6 copy-start.13

commit v2 on v0

--- a/solution.py
+++ b/solution.py
@@ -15,7 +15,7 @@
 
 COLS = 4
 SENT_K = ((4, 3), (5, 6))
-SENT_V = ((5,), (3,), (7,))
+SENT_V = ((5,), (3, 7))
 KEPT_K = ((2,), (7,), (0,), (1,))
 KEPT_V = ((1,), (4,), (2,), (6,), (0,))
 
@@ -146,15 +146,15 @@
     return k0n + from_right[per:] + a2 + crossed
 
 
-def move_values(got2, got1, got3, y0, groups):
+def move_values(got2, got, y0, groups):
     v2n, v1n, v3n, v0n = groups
     per = v1n.shape[0]
     cut = per // 2
     from_left = right(v2n[:cut] + got2[:cut])
     from_right = left(v2n[cut:] + got2[cut:])
     rest = jnp.zeros((per - cut,) + v1n.shape[1:], v1n.dtype)
-    a2 = right(v1n + got1 + jnp.concatenate([from_left, rest]))
-    b2 = left(v3n + got3 + jnp.concatenate([rest, from_right]))
+    a2 = right(v1n + got[:per] + jnp.concatenate([from_left, rest]))
+    b2 = left(v3n + got[per:] + jnp.concatenate([rest, from_right]))
     return v0n + y0 + a2 + b2
 
 
@@ -435,8 +435,7 @@
     far2 = across(out_v[0])
     from_left = right(out_k[0])
     from_right = left(out_k[1])
-    far1 = across(out_v[1])
-    far3 = across(out_v[2])
+    far = across(out_v[1])
     kept_k, kept_v = out_k[len(SENT_K) :], out_v[len(SENT_V) :]
     near = across(kept_v[0])
     packet = attend(
@@ -445,7 +444,7 @@
     )
     packet, rest_k, rest_v = lax.optimization_barrier((packet, kept_k, kept_v[1:]))
     moved_keys = move_keys(from_left, from_right, rest_k).reshape(shape)
-    moved_values = move_values(far2, far1, far3, near, rest_v).reshape(shape)
+    moved_values = move_values(far2, far, near, rest_v).reshape(shape)
     got = spread(packet)
     mine = join(got, rows, queries.shape[1], queries.shape[2])
     attended = spread(mine).reshape(queries.shape)

time: 116 us -> 115 us (level)
  starting transfers between devices: 41.7 us -> 38.4 us
  waiting for transfers between devices: 44.7 us -> 47.7 us
    ppermute x4, waiting for transfers between devices: 23.6 us -> 3.97 us  [right(): return lax.ppermute(x, 'inst', route)]
    ppermute x5 -> x4, waiting for transfers between devices: 21.1 us -> 38 us  [across(): lax.ppermute(x, 'inst', [(i, i ^ COLS) for i in range(lax.axis_size('inst...]
    ppermute x4, waiting for transfers between devices: 0.01 us -> 5.8 us  [left(): return lax.ppermute(x, 'inst', route)]
    ppermute x5 -> x4, starting transfers between devices: 14.2 us -> 10.6 us  [across(): lax.ppermute(x, 'inst', [(i, i ^ COLS) for i in range(lax.axis_size('inst...]
    add x2 -> x1, other arithmetic: 2.79 us -> 2.34 us  [move_values(): a2 = right(v1n + got[:per] + jnp.concatenate([from_left, rest]))]
  transfers between devices with their start and end apart: 17 -> 16, of which waited for: 4 -> 5; matrix products, arithmetic and copies ran while one was open for 11% -> 10% of each run, Pallas kernels for 12% -> 12%
where the time goes in v2:
time: 115 us; the launch traced here: 114 us
  waiting for transfers between devices  47.7 us (41%)
  starting transfers between devices  38.4 us (33%)
  Pallas kernels  13.6 us (12%)
  other arithmetic  11.8 us (10%)
  local copies, waits for them, and re-layouts  2.01 us (2%)
    ppermute x4, waiting for transfers between devices, across(): lax.ppermute(x, 'inst', [(i, i ^ COLS) for i in range(lax.axis_size('inst...  38 us
    all_to_all x2, starting transfers between devices, spread(): return lax.all_to_all(x, 'inst', split_axis=0, concat_axis=0, tiled=True)  15.8 us
    ppermute x4, starting transfers between devices, across(): lax.ppermute(x, 'inst', [(i, i ^ COLS) for i in range(lax.axis_size('inst...  10.6 us
    ppermute x4, starting transfers between devices, left(): return lax.ppermute(x, 'inst', route)  7.2 us
    pallas_call x1, Pallas kernels, attend(): pl.pallas_call(attend_body, in_specs=[smem] * 3 + [anyspace] * 7, out_spe...  5.87 us
    ppermute x4, waiting for transfers between devices, left(): return lax.ppermute(x, 'inst', route)  5.8 us
    ppermute x4, starting transfers between devices, right(): return lax.ppermute(x, 'inst', route)  4.21 us
    pallas_call x1, Pallas kernels, pack(): pl.pallas_call(functools.partial(pack_body, groups_k, groups_v), in_specs...  4.2 us
  transfers between devices with their start and end apart: 16, of which 5 were waited for; matrix products, arithmetic and copies ran while one was open for 10% of the time, Pallas kernels for 12%

profile of v2, /device:TPU:0, one launch (start us, length us, event | category | flops | bytes accessed | tf_op | source)
XLA Modules:
  0.0 114.2 jit_solution(13213534921311623482)
XLA Ops:
  0.6 0.1 collective-permute-start
  0.7 0.5 collective-permute-start.1
  1.2 0.6 compare_select_fusion.4.base.meta
  1.8 4.2 %shard_map.103 = (bf16[64,64,128]{2,1,0:T(8,128)(2,1)}, bf16[64,64,128]{2,1,0:T(8,128)(2,1)}, bf16[32,64,128]{2,1,0:T(8,128)(2,1)}, bf16[32,64,128]{2,1,0:T(8,12...) custom-call(s32[128]{0:T(128)} %old_block.3, ...), custom_call_target="tpu_custom_call" | custom-call | tf_op jit(solution)/shard_map/pallas_call | solution.py:104
  6.0 2.9 %collective-permute-start.2 = (bf16[64,64,128]{2,1,0:T(8,128)(2,1)}, bf16[64,64,128]{2,1,0:T(8,128)(2,1)S(1)}, u32[]{:S(2)}, u32[]{:S(2)}) collective-permute-start(bf16[64,64,128]{2,1,0:T(8,128)(2,1)} %get-tuple-element.64), channel_id=1, source_target_pairs={{16,0},{32,16},{48,32},{0,48},{80,64},{96,80},{112,96},{64,112},{1... | collective-permute-start | bytes 3145736 | tf_op jit(solution)/shard_map/ppermute | solution.py:132
  8.9 3.2 %collective-permute-start.8 = (bf16[64,64,128]{2,1,0:T(8,128)(2,1)}, bf16[64,64,128]{2,1,0:T(8,128)(2,1)}, u32[]{:S(2)}, u32[]{:S(2)}) collective-permute-start(bf16[64,64,128]{2,1,0:T(8,128)(2,1)} %get-tuple-element.74), channel_id=1, source_target_pairs={{0,64},{16,80},{32,96},{48,112},{64,0},{80,16},{96,32},{112,48},{1... | collective-permute-start | bytes 3145736 | tf_op jit(solution)/shard_map/ppermute | solution.py:136
  12.1 0.3 collective-permute-start.9
  12.5 0.0 collective-permute-done.ok
  12.5 1.0 collective-permute-start.3
  13.5 0.0 collective-permute-done.1.ov
  13.5 3.5 %collective-permute-start.7 = (bf16[32,64,128]{2,1,0:T(8,128)(2,1)}, bf16[32,64,128]{2,1,0:T(8,128)(2,1)}, u32[]{:S(2)}, u32[]{:S(2)}) collective-permute-start(bf16[32,64,128]{2,1,0:T(8,128)(2,1)} %get-tuple-element.72), channel_id=1, source_target_pairs={{0,64},{16,80},{32,96},{48,112},{64,0},{80,16},{96,32},{112,48},{1... | collective-permute-start | bytes 1572872 | tf_op jit(solution)/shard_map/ppermute | solution.py:136
  16.9 0.0 copy-done.1
  16.9 5.9 %attend.1 = bf16[8,528,128]{2,1,0:T(8,128)(2,1)} custom-call(s32[128]{0:T(128)} %old_block.3, s32[64]{0:T(128)} %lengths.1, s32[16]{0:T(128)} %compare_select_fusion.4.base.meta, bf16[64,16,512]{2,1,0:T(8,128)(2,1)} %q, bf16[128,64,128]{2,1,0:T(8,128)(2,1)} %bitcast.13, bf16[128,64,128]{2,1,0:T(8,128)(2,1)} %bitcast.16, bf16[128,64,128]{2,1,0:T(8,128)(2,1)} %copy-done.1, ...), custom_call_target="tpu_custom_call" | custom-call | tf_op jit(solution)/shard_map/attend/pallas_call | solution.py:335
  22.8 0.0 copy-start.7
  22.8 8.2 %all-to-all-start = ((bf16[8,528,128]{2,1,0:T(8,128)(2,1)}), bf16[8,528,128]{2,1,0:T(8,128)(2,1)S(1)}, u32[]{:S(2)}, u32[]{:S(2)}) async-start(bf16[8,528,128]{2,1,0:T(8,128)(2,1)} %attend.1), calls=%async_computation | async-start | bytes 2162688 | tf_op jit(solution)/shard_map/all_to_all | solution.py:412
  31.1 25.6 %collective-permute-done.9 = bf16[32,64,128]{2,1,0:T(8,128)(2,1)} collective-permute-done((bf16[32,64,128]{2,1,0:T(8,128)(2,1)}, bf16[32,64,128]{2,1,0:T(8,128)(2,1)}, u32[]{:S(2)}, u32[]{:S(2)}) %collective-permute-start.9) | collective-permute-done | bytes 524320 | tf_op jit(solution)/shard_map/ppermute | solution.py:136
  56.7 1.2 %slice_add_fusion.6 = (bf16[16,64,128]{2,1,0:T(8,128)(2,1)S(1)}, bf16[16,64,128]{2,1,0:T(8,128)(2,1)S(1)}) fusion(bf16[32,64,128]{2,1,0:T(8,128)(2,1)} %collective-permute-done.9, bf16[32,64,128]{2,1,0:T(8,128)(2,1)} %get-tuple-element.75), kind=kLoop, calls=%fused_computation.13 | loop fusion | flops 262144 | bytes 1572864 | tf_op jit(solution)/shard_map/add | solution.py:153
  57.9 1.0 collective-permute-start.10
  59.0 0.0 collective-permute-done.2
  59.0 2.3 %collective-permute-start.12 = (bf16[16,64,128]{2,1,0:T(8,128)(2,1)S(1)}, bf16[16,64,128]{2,1,0:T(8,128)(2,1)S(1)}, u32[]{:S(2)}, u32[]{:S(2)}) collective-permute-start(bf16[16,64,128]{2,1,0:T(8,128)(2,1)S(1)} %get-tuple-element.85), channel_id=1, source_target_pairs={{16,0},{32,16},{48,32},{0,48},{80,64},{96,80},{112,96},{64,112},{1... | collective-permute-start | bytes 786440 | tf_op jit(solution)/shard_map/ppermute | solution.py:132
  61.3 0.1 slice_add_fusion.2
  61.3 0.0 copy-start.4
  61.3 0.0 collective-permute-done.8
  61.3 0.3 collective-permute-start.5
  61.6 4.0 %collective-permute-done.10 = bf16[16,64,128]{2,1,0:T(8,128)(2,1)S(1)} collective-permute-done((bf16[16,64,128]{2,1,0:T(8,128)(2,1)S(1)}, bf16[16,64,128]{2,1,0:T(8,128)(2,1)S(1)}, u32[]{:S(2)}, u32[]{:S(2)}) %collective-permute-start.10) | collective-permute-done | bytes 262176 | tf_op jit(solution)/shard_map/ppermute | solution.py:126
  65.6 2.5 %collective-permute-done.12 = bf16[16,64,128]{2,1,0:T(8,128)(2,1)S(1)} collective-permute-done((bf16[16,64,128]{2,1,0:T(8,128)(2,1)S(1)}, bf16[16,64,128]{2,1,0:T(8,128)(2,1)S(1)}, u32[]{:S(2)}, u32[]{:S(2)}) %collective-permute-start.12) | collective-permute-done | bytes 262176 | tf_op jit(solution)/shard_map/ppermute | solution.py:132
  68.1 2.3 %fusion.1 = (bf16[32,64,128]{2,1,0:T(8,128)(2,1)}, bf16[32,64,128]{2,1,0:T(8,128)(2,1)}) fusion(bf16[32,64,128]{2,1,0:T(8,128)(2,1)S(1)} %copy-done.5, bf16[64,64,128]{2,1,0:T(8,128)(2,1)} %collective-permute-done.8, bf16[16,64,128]{2,1,0:T(8,128)(2,1)S(1)} %collective-permute-done.10, bf16[16,64,128]{2,1,0:T(8,128)(2,1)S(1)} %collective-permute-done.12, ...), kind=kLoop, calls=%fused_computation.3 | loop fusion | flops 1048576 | bytes 3670016 | tf_op jit(solution)/shard_map/add | solution.py:156
  70.5 1.8 %collective-permute-start.11 = (bf16[32,64,128]{2,1,0:T(8,128)(2,1)}, bf16[32,64,128]{2,1,0:T(8,128)(2,1)}, u32[]{:S(2)}, u32[]{:S(2)}) collective-permute-start(bf16[32,64,128]{2,1,0:T(8,128)(2,1)} %get-tuple-element.82), channel_id=1, source_target_pairs={{0,16},{16,32},{32,48},{48,0},{64,80},{80,96},{96,112},{112,64},{1... | collective-permute-start | bytes 1572872 | tf_op jit(solution)/shard_map/ppermute | solution.py:126
  72.3 1.7 %collective-permute-start.13 = (bf16[32,64,128]{2,1,0:T(8,128)(2,1)}, bf16[32,64,128]{2,1,0:T(8,128)(2,1)}, u32[]{:S(2)}, u32[]{:S(2)}) collective-permute-start(bf16[32,64,128]{2,1,0:T(8,128)(2,1)} %get-tuple-element.83), channel_id=1, source_target_pairs={{16,0},{32,16},{48,32},{0,48},{80,64},{96,80},{112,96},{64,112},{1... | collective-permute-start | bytes 1572872 | tf_op jit(solution)/shard_map/ppermute | solution.py:132
  74.0 0.0 collective-permute-done.3
  74.0 1.9 %slice_add_fusion.3 = bf16[32,64,128]{2,1,0:T(8,128)(2,1)} fusion(bf16[32,64,128]{2,1,0:T(8,128)(2,1)S(1)} %copy-done.4, bf16[64,64,128]{2,1,0:T(8,128)(2,1)} %collective-permute-done.3), kind=kLoop, calls=%fused_computation.5 | loop fusion | flops 262144 | bytes 1572864 | tf_op jit(solution)/shard_map/add | solution.py:142
  75.9 0.3 collective-permute-start.4
  76.2 3.2 %collective-permute-done.5 = bf16[32,64,128]{2,1,0:T(8,128)(2,1)} collective-permute-done((bf16[32,64,128]{2,1,0:T(8,128)(2,1)S(1)}, bf16[32,64,128]{2,1,0:T(8,128)(2,1)}, u32[]{:S(2)}, u32[]{:S(2)}) %collective-permute-start.5) | collective-permute-done | bytes 524320 | tf_op jit(solution)/shard_map/ppermute | solution.py:132
  79.5 0.0 all-to-all-done.arrived
  79.5 1.0 copy-done
  80.5 3.5 %join.1 = bf16[8,8,16,512]{3,2,1,0:T(8,128)(2,1)} custom-call(bf16[8,528,128]{2,1,0:T(8,128)(2,1)} %copy-done), custom_call_target="tpu_custom_call" | custom-call | tf_op jit(solution)/shard_map/join/pallas_call | solution.py:401
  84.0 7.5 %all-to-all-start.1 = ((bf16[8,8,16,512]{3,2,1,0:T(8,128)(2,1)}), bf16[8,8,16,512]{3,2,1,0:T(8,128)(2,1)S(1)}, u32[]{:S(2)}, u32[]{:S(2)}) async-start(bf16[8,8,16,512]{3,2,1,0:T(8,128)(2,1)} %join.1), calls=%async_computation.1 | async-start | bytes 2097152 | tf_op jit(solution)/shard_map/all_to_all | solution.py:412
  91.6 1.5 %add_add_fusion = bf16[32,64,128]{2,1,0:T(8,128)(2,1)S(1)} fusion(bf16[32,64,128]{2,1,0:T(8,128)(2,1)} %collective-permute-done.5, bf16[32,64,128]{2,1,0:T(8,128)(2,1)} %get-tuple-element.67, bf16[64,64,128]{2,1,0:T(8,128)(2,1)} %collective-permute-done.3), kind=kLoop, calls=%fused_computation.11 | loop fusion | flops 524288 | bytes 2097152 | tf_op jit(solution)/shard_map/add | solution.py:145
  93.1 3.6 %collective-permute-start.6 = (bf16[32,64,128]{2,1,0:T(8,128)(2,1)S(1)}, bf16[32,64,128]{2,1,0:T(8,128)(2,1)S(1)}, u32[]{:S(2)}, u32[]{:S(2)}) collective-permute-start(bf16[32,64,128]{2,1,0:T(8,128)(2,1)S(1)} %add_add_fusion), channel_id=1, source_target_pairs={{0,64},{16,80},{32,96},{48,112},{64,0},{80,16},{96,32},{112,48},{1... | collective-permute-start | bytes 1572872 | tf_op jit(solution)/shard_map/ppermute | solution.py:136
  96.7 0.0 collective-permute-done.7
  96.7 0.0 collective-permute-done.11
  96.7 0.0 collective-permute-done.13
  96.7 2.3 %add_bitcast_fusion = bf16[32,1,64,128]{3,2,1,0:T(8,128)(2,1)} fusion(bf16[32,64,128]{2,1,0:T(8,128)(2,1)} %collective-permute-done.13, bf16[32,64,128]{2,1,0:T(8,128)(2,1)} %collective-permute-done.11, bf16[32,64,128]{2,1,0:T(8,128)(2,1)S(1)} %copy-done.3, bf16[32,64,128]{2,1,0:T(8,128)(2,1)} %collective-permute-done.7), kind=kLoop, calls=%fused_computation.10 | loop fusion | flops 786432 | bytes 2621440
  99.0 0.0 collective-permute-done.4
  99.0 12.3 %collective-permute-done.6 = bf16[32,64,128]{2,1,0:T(8,128)(2,1)S(1)} collective-permute-done((bf16[32,64,128]{2,1,0:T(8,128)(2,1)S(1)}, bf16[32,64,128]{2,1,0:T(8,128)(2,1)S(1)}, u32[]{:S(2)}, u32[]{:S(2)}) %collective-permute-start.6) | collective-permute-done | bytes 524320 | tf_op jit(solution)/shard_map/ppermute | solution.py:136
  111.3 1.9 %fusion.4 = bf16[32,1,64,128]{3,2,1,0:T(8,128)(2,1)} fusion(bf16[32,64,128]{2,1,0:T(8,128)(2,1)S(1)} %collective-permute-done.6, bf16[32,64,128]{2,1,0:T(8,128)(2,1)} %collective-permute-done.4, bf16[32,64,128]{2,1,0:T(8,128)(2,1)S(1)} %copy-done.2, bf16[64,64,128]{2,1,0:T(8,128)(2,1)S(1)} %collective-permute-done.2), kind=kLoop, calls=%fused_computation.9 | loop fusion | flops 786432 | bytes 2621440
  113.2 0.0 all-to-all-done.1
  113.2 1.0 copy.14
  (12 shorter events, 0.0 us)
Async XLA Ops:
  0.6 11.8 %collective-permute-start = (bf16[128,64,128]{2,1,0:T(8,128)(2,1)}, bf16[128,64,128]{2,1,0:T(8,128)(2,1)S(1)}, u32[]{:S(2)}, u32[]{:S(2)}) collective-permute-start(bf16[128,64,128]{2,1,0:T(8,128)(2,1)} %bitcast.11), channel_id=1, source_target_pairs={{0,1},{1,0},{2,3},{3,2},{4,5},{5,4},{6,7},{7,6},{8,9},{9,8},{10,11... | collective-permute-start | bytes 6291464 | tf_op jit(solution)/shard_map/ppermute | solution.py:426
  0.7 12.8 %collective-permute-start.1 = (bf16[128,64,128]{2,1,0:T(8,128)(2,1)}, bf16[128,64,128]{2,1,0:T(8,128)(2,1)}, u32[]{:S(2)}, u32[]{:S(2)}) collective-permute-start(bf16[128,64,128]{2,1,0:T(8,128)(2,1)} %bitcast.14), channel_id=1, source_target_pairs={{0,1},{1,0},{2,3},{3,2},{4,5},{5,4},{6,7},{7,6},{8,9},{9,8},{10,11... | collective-permute-start | bytes 6291464 | tf_op jit(solution)/shard_map/ppermute | solution.py:427
  6.0 53.0 %collective-permute-start.2 = (bf16[64,64,128]{2,1,0:T(8,128)(2,1)}, bf16[64,64,128]{2,1,0:T(8,128)(2,1)S(1)}, u32[]{:S(2)}, u32[]{:S(2)}) collective-permute-start(bf16[64,64,128]{2,1,0:T(8,128)(2,1)} %get-tuple-element.64), channel_id=1, source_target_pairs={{16,0},{32,16},{48,32},{0,48},{80,64},{96,80},{112,96},{64,112},{1... | collective-permute-start | bytes 3145736 | tf_op jit(solution)/shard_map/ppermute | solution.py:132
  8.9 52.4 %collective-permute-start.8 = (bf16[64,64,128]{2,1,0:T(8,128)(2,1)}, bf16[64,64,128]{2,1,0:T(8,128)(2,1)}, u32[]{:S(2)}, u32[]{:S(2)}) collective-permute-start(bf16[64,64,128]{2,1,0:T(8,128)(2,1)} %get-tuple-element.74), channel_id=1, source_target_pairs={{0,64},{16,80},{32,96},{48,112},{64,0},{80,16},{96,32},{112,48},{1... | collective-permute-start | bytes 3145736 | tf_op jit(solution)/shard_map/ppermute | solution.py:136
  12.1 44.6 %collective-permute-start.9 = (bf16[32,64,128]{2,1,0:T(8,128)(2,1)}, bf16[32,64,128]{2,1,0:T(8,128)(2,1)}, u32[]{:S(2)}, u32[]{:S(2)}) collective-permute-start(bf16[32,64,128]{2,1,0:T(8,128)(2,1)} %get-tuple-element.76), channel_id=1, source_target_pairs={{0,64},{16,80},{32,96},{48,112},{64,0},{80,16},{96,32},{112,48},{1... | collective-permute-start | bytes 1572872 | tf_op jit(solution)/shard_map/ppermute | solution.py:136
  12.5 4.5 %copy-start.1 = (bf16[128,64,128]{2,1,0:T(8,128)(2,1)}, bf16[128,64,128]{2,1,0:T(8,128)(2,1)S(1)}, u32[]{:S(2)}) copy-start(bf16[128,64,128]{2,1,0:T(8,128)(2,1)S(1)} %collective-permute-done.ok) | copy-start | bytes 6291460
  12.5 61.5 %collective-permute-start.3 = (bf16[64,64,128]{2,1,0:T(8,128)(2,1)}, bf16[64,64,128]{2,1,0:T(8,128)(2,1)}, u32[]{:S(2)}, u32[]{:S(2)}) collective-permute-start(bf16[64,64,128]{2,1,0:T(8,128)(2,1)} %get-tuple-element.66), channel_id=1, source_target_pairs={{0,16},{16,32},{32,48},{48,0},{64,80},{80,96},{96,112},{112,64},{1... | collective-permute-start | bytes 3145736 | tf_op jit(solution)/shard_map/ppermute | solution.py:126
  13.5 83.2 %collective-permute-start.7 = (bf16[32,64,128]{2,1,0:T(8,128)(2,1)}, bf16[32,64,128]{2,1,0:T(8,128)(2,1)}, u32[]{:S(2)}, u32[]{:S(2)}) collective-permute-start(bf16[32,64,128]{2,1,0:T(8,128)(2,1)} %get-tuple-element.72), channel_id=1, source_target_pairs={{0,64},{16,80},{32,96},{48,112},{64,0},{80,16},{96,32},{112,48},{1... | collective-permute-start | bytes 1572872 | tf_op jit(solution)/shard_map/ppermute | solution.py:136
  22.8 38.4 %copy-start.7 = (bf16[32,64,128]{2,1,0:T(8,128)(2,1)S(1)}, bf16[32,64,128]{2,1,0:T(8,128)(2,1)}, u32[]{:S(2)}) copy-start(bf16[32,64,128]{2,1,0:T(8,128)(2,1)} %get-tuple-element.68) | copy-start | bytes 1572868
  22.8 56.7 %all-to-all-start = ((bf16[8,528,128]{2,1,0:T(8,128)(2,1)}), bf16[8,528,128]{2,1,0:T(8,128)(2,1)S(1)}, u32[]{:S(2)}, u32[]{:S(2)}) async-start(bf16[8,528,128]{2,1,0:T(8,128)(2,1)} %attend.1), calls=%async_computation | async-start | bytes 2162688 | tf_op jit(solution)/shard_map/all_to_all | solution.py:412
  31.1 37.1 %copy-start.5 = (bf16[32,64,128]{2,1,0:T(8,128)(2,1)S(1)}, bf16[32,64,128]{2,1,0:T(8,128)(2,1)}, u32[]{:S(2)}) copy-start(bf16[32,64,128]{2,1,0:T(8,128)(2,1)} %get-tuple-element.73) | copy-start | bytes 1572868
  31.1 37.1 %copy-start.6 = (bf16[32,64,128]{2,1,0:T(8,128)(2,1)S(1)}, bf16[32,64,128]{2,1,0:T(8,128)(2,1)}, u32[]{:S(2)}) copy-start(bf16[32,64,128]{2,1,0:T(8,128)(2,1)} %get-tuple-element.77) | copy-start | bytes 1572868
  57.9 7.7 %collective-permute-start.10 = (bf16[16,64,128]{2,1,0:T(8,128)(2,1)S(1)}, bf16[16,64,128]{2,1,0:T(8,128)(2,1)S(1)}, u32[]{:S(2)}, u32[]{:S(2)}) collective-permute-start(bf16[16,64,128]{2,1,0:T(8,128)(2,1)S(1)} %get-tuple-element.84), channel_id=1, source_target_pairs={{0,16},{16,32},{32,48},{48,0},{64,80},{80,96},{96,112},{112,64},{1... | collective-permute-start | bytes 786440 | tf_op jit(solution)/shard_map/ppermute | solution.py:126
  59.0 9.2 %collective-permute-start.12 = (bf16[16,64,128]{2,1,0:T(8,128)(2,1)S(1)}, bf16[16,64,128]{2,1,0:T(8,128)(2,1)S(1)}, u32[]{:S(2)}, u32[]{:S(2)}) collective-permute-start(bf16[16,64,128]{2,1,0:T(8,128)(2,1)S(1)} %get-tuple-element.85), channel_id=1, source_target_pairs={{16,0},{32,16},{48,32},{0,48},{80,64},{96,80},{112,96},{64,112},{1... | collective-permute-start | bytes 786440 | tf_op jit(solution)/shard_map/ppermute | solution.py:132
  61.3 12.7 %copy-start.4 = (bf16[32,64,128]{2,1,0:T(8,128)(2,1)S(1)}, bf16[32,64,128]{2,1,0:T(8,128)(2,1)}, u32[]{:S(2)}) copy-start(bf16[32,64,128]{2,1,0:T(8,128)(2,1)} %get-tuple-element.65) | copy-start | bytes 1572868
  61.3 18.1 %collective-permute-start.5 = (bf16[32,64,128]{2,1,0:T(8,128)(2,1)S(1)}, bf16[32,64,128]{2,1,0:T(8,128)(2,1)}, u32[]{:S(2)}, u32[]{:S(2)}) collective-permute-start(bf16[32,64,128]{2,1,0:T(8,128)(2,1)S(1)} %slice_add_fusion.2), channel_id=1, source_target_pairs={{16,0},{32,16},{48,32},{0,48},{80,64},{96,80},{112,96},{64,112},{1... | collective-permute-start | bytes 1572872 | tf_op jit(solution)/shard_map/ppermute | solution.py:132
  70.5 26.2 %collective-permute-start.11 = (bf16[32,64,128]{2,1,0:T(8,128)(2,1)}, bf16[32,64,128]{2,1,0:T(8,128)(2,1)}, u32[]{:S(2)}, u32[]{:S(2)}) collective-permute-start(bf16[32,64,128]{2,1,0:T(8,128)(2,1)} %get-tuple-element.82), channel_id=1, source_target_pairs={{0,16},{16,32},{32,48},{48,0},{64,80},{80,96},{96,112},{112,64},{1... | collective-permute-start | bytes 1572872 | tf_op jit(solution)/shard_map/ppermute | solution.py:126
  72.3 24.4 %collective-permute-start.13 = (bf16[32,64,128]{2,1,0:T(8,128)(2,1)}, bf16[32,64,128]{2,1,0:T(8,128)(2,1)}, u32[]{:S(2)}, u32[]{:S(2)}) collective-permute-start(bf16[32,64,128]{2,1,0:T(8,128)(2,1)} %get-tuple-element.83), channel_id=1, source_target_pairs={{16,0},{32,16},{48,32},{0,48},{80,64},{96,80},{112,96},{64,112},{1... | collective-permute-start | bytes 1572872 | tf_op jit(solution)/shard_map/ppermute | solution.py:132
  75.9 23.1 %collective-permute-start.4 = (bf16[32,64,128]{2,1,0:T(8,128)(2,1)}, bf16[32,64,128]{2,1,0:T(8,128)(2,1)}, u32[]{:S(2)}, u32[]{:S(2)}) collective-permute-start(bf16[32,64,128]{2,1,0:T(8,128)(2,1)} %slice_add_fusion.3), channel_id=1, source_target_pairs={{0,16},{16,32},{32,48},{48,0},{64,80},{80,96},{96,112},{112,64},{1... | collective-permute-start | bytes 1572872 | tf_op jit(solution)/shard_map/ppermute | solution.py:126
  79.5 1.0 copy-start
  84.0 12.7 %copy-start.3 = (bf16[32,64,128]{2,1,0:T(8,128)(2,1)S(1)}, bf16[32,64,128]{2,1,0:T(8,128)(2,1)}, u32[]{:S(2)}) copy-start(bf16[32,64,128]{2,1,0:T(8,128)(2,1)} %get-tuple-element.71) | copy-start | bytes 1572868
  84.0 29.2 %all-to-all-start.1 = ((bf16[8,8,16,512]{3,2,1,0:T(8,128)(2,1)}), bf16[8,8,16,512]{3,2,1,0:T(8,128)(2,1)S(1)}, u32[]{:S(2)}, u32[]{:S(2)}) async-start(bf16[8,8,16,512]{3,2,1,0:T(8,128)(2,1)} %join.1), calls=%async_computation.1 | async-start | bytes 2097152 | tf_op jit(solution)/shard_map/all_to_all | solution.py:412
  91.6 19.7 %copy-start.2 = (bf16[32,64,128]{2,1,0:T(8,128)(2,1)S(1)}, bf16[32,64,128]{2,1,0:T(8,128)(2,1)}, u32[]{:S(2)}) copy-start(bf16[32,64,128]{2,1,0:T(8,128)(2,1)} %get-tuple-element.63) | copy-start | bytes 1572868
  93.1 18.2 %collective-permute-start.6 = (bf16[32,64,128]{2,1,0:T(8,128)(2,1)S(1)}, bf16[32,64,128]{2,1,0:T(8,128)(2,1)S(1)}, u32[]{:S(2)}, u32[]{:S(2)}) collective-permute-start(bf16[32,64,128]{2,1,0:T(8,128)(2,1)S(1)} %add_add_fusion), channel_id=1, source_target_pairs={{0,64},{16,80},{32,96},{48,112},{64,0},{80,16},{96,32},{112,48},{1... | collective-permute-start | bytes 1572872 | tf_op jit(solution)/shard_map/ppermute | solution.py:136
